TPU v7x, 8 devices: a whole 2x2x1 slice. The times are simulated.
8 devices in a mesh: rep: 1 (over z), dp: 8 (over x, y, core).
Axes of the slice: x: 2, y: 2, z: 1, core: 2. Of those that a mesh axis runs over, the one named last changes fastest.
Arguments:
- x: bfloat16 [8, 2048, 768], P(('rep', 'dp'))
- dy: bfloat16 [8, 2048, 768], P(('rep', 'dp'))
- w_gate: bfloat16 [2, 768, 3072], replicated
- w_up: bfloat16 [2, 768, 3072], replicated
- w_down: bfloat16 [2, 3072, 768], replicated
- m_w_gate: float32 [2, 768, 3072], P(None, 'dp')
- m_w_up: float32 [2, 768, 3072], P(None, 'dp')
- m_w_down: float32 [2, 3072, 768], P(None, 'dp')
- v_w_gate: float32 [2, 768, 3072], P(None, 'dp')
- v_w_up: float32 [2, 768, 3072], P(None, 'dp')
- v_w_down: float32 [2, 3072, 768], P(None, 'dp')
Outputs:
- output 1: bfloat16 [2, 768, 3072], P('rep')
- output 2: bfloat16 [2, 768, 3072], P('rep')
- output 3: bfloat16 [2, 3072, 768], P('rep')
- output 4: float32 [2, 768, 3072], P('rep', 'dp')
- output 5: float32 [2, 768, 3072], P('rep', 'dp')
- output 6: float32 [2, 3072, 768], P('rep', 'dp')
- output 7: float32 [2, 768, 3072], P('rep', 'dp')
- output 8: float32 [2, 768, 3072], P('rep', 'dp')
- output 9: float32 [2, 3072, 768], P('rep', 'dp')
All inputs are finite; a program needn't handle non-finite values.
Results may differ from a plain program's by a relative error of at most 0.0228.
Values are sent between devices in bfloat16 or wider.
A program may use at most 2 GiB of HBM per device.

v0:
```python
import jax
import jax.numpy as jnp
from jax import lax

NAMES = ("w_gate", "w_up", "w_down")


def matmul(a, w):
    return jnp.dot(a, w, preferred_element_type=jnp.float32).astype(jnp.bfloat16)


def normed(h):
    wide = h.astype(jnp.float32)
    scale = lax.rsqrt(jnp.mean(wide**2, -1, keepdims=True) + 1e-6)
    return (wide * scale).astype(jnp.bfloat16)


def layer(h, w):
    a = normed(h)
    gate = jnp.dot(a, w["w_gate"], preferred_element_type=jnp.float32)
    up = jnp.dot(a, w["w_up"], preferred_element_type=jnp.float32)
    return h + matmul((jax.nn.silu(gate) * up).astype(jnp.bfloat16), w["w_down"])


def adamw(w, m, v, g):
    m = 0.9 * m + 0.1 * g
    v = 0.95 * v + 0.05 * g * g
    step = m * lax.rsqrt(v + 1e-8) + 0.1 * w
    return (w - 0.02 * step).astype(jnp.bfloat16), m, v


def stack(weights, h):
    for number in range(weights["w_gate"].shape[0]):
        h = layer(h, {name: w[number] for name, w in weights.items()})
    return h


def solution(mesh):
    groups = mesh.shape["rep"]

    def step(x, dy, *arrays):
        weights, m, v = (arrays[i : i + 3] for i in (0, 3, 6))
        x, dy = (t.reshape(groups, -1, *t.shape[1:]) for t in (x, dy))

        def of_a_group(x, dy):
            _, back = jax.vjp(lambda w: stack(w, x), dict(zip(NAMES, weights, strict=True)))
            by_weights = back(dy)[0]
            gradients = [by_weights[name].astype(jnp.float32) for name in NAMES]
            new = [adamw(w.astype(jnp.float32), m, v, g) for w, m, v, g in zip(weights, m, v, gradients, strict=True)]
            return tuple(one[which] for which in range(3) for one in new)

        return tuple(t.reshape(-1, *t.shape[2:]) for t in jax.vmap(of_a_group)(x, dy))

    return step
```

profile of v0, /device:TPU:0, one launch (start us, length us, event | category | flops | bytes accessed | tf_op | source)
XLA Modules:
  0.0 833.0 jit_solution(16422940975876191675)
XLA Ops:
  14.6 16.0 %fusion.54 = f32[2048,3072]{1,0:T(8,128)} fusion(bf16[2,768,3072]{2,1,0:T(8,128)(2,1)} %param, bf16[1,2048,768]{2,1,0:T(8,128)(2,1)S(1)} %copy-done.1, f32[2048]{0:T(1024)S(1)} %add_rsqrt_fusion), kind=kOutput, calls=%fused_computation.71 | convolution fusion | flops 9668395008 | bytes 33038336 | tf_op jit(solution)/vmap(jvp())/dot_general | solution.py:20
  30.6 15.9 %fusion.52 = f32[2048,3072]{1,0:T(8,128)} fusion(bf16[2,768,3072]{2,1,0:T(8,128)(2,1)} %param.5, bf16[1,2048,768]{2,1,0:T(8,128)(2,1)S(1)} %copy-done.1, f32[2048]{0:T(1024)S(1)} %add_rsqrt_fusion), kind=kOutput, calls=%fused_computation.69 | convolution fusion | flops 9668395008 | bytes 33038336 | tf_op jit(solution)/vmap(jvp())/dot_general | solution.py:21
  46.5 21.8 %fusion.26 = bf16[2048,3072]{1,0:T(8,128)(2,1)} fusion(f32[2048,3072]{1,0:T(8,128)} %fusion.52, f32[2048,3072]{1,0:T(8,128)} %fusion.54), kind=kLoop, calls=%fused_computation.35 | loop fusion | flops 37748736 | bytes 62914560
  68.3 15.0 %fusion.39 = (f32[2048]{0:T(1024)S(1)}, bf16[1,2048,768]{1,2,0:T(8,128)(2,1)S(1)}) fusion(bf16[1,2048,768]{1,2,0:T(8,128)(2,1)S(1)} %copy-done.5, bf16[2048,3072]{1,0:T(8,128)(2,1)} %fusion.26, bf16[2,3072,768]{2,1,0:T(8,128)(2,1)} %param.3), kind=kOutput, calls=%fused_computation.56 | convolution fusion | flops 9671538688 | bytes 23601152 | tf_op jit(solution)/vmap(jvp())/dot_general | solution.py:9
  84.1 16.0 %fusion.42 = f32[2048,3072]{1,0:T(8,128)} fusion(bf16[2,768,3072]{2,1,0:T(8,128)(2,1)} %param, bf16[1,2048,768]{1,2,0:T(8,128)(2,1)S(1)} %get-tuple-element.10, f32[2048]{0:T(1024)S(1)} %bitcast.334), kind=kOutput, calls=%fused_computation.59 | convolution fusion | flops 9668395008 | bytes 33038336 | tf_op jit(solution)/vmap(jvp())/dot_general | solution.py:20
  100.1 16.0 %fusion.46 = f32[2048,3072]{1,0:T(8,128)} fusion(bf16[2,768,3072]{2,1,0:T(8,128)(2,1)} %param.5, bf16[1,2048,768]{1,2,0:T(8,128)(2,1)S(1)} %get-tuple-element.10, f32[2048]{0:T(1024)S(1)} %bitcast.335), kind=kOutput, calls=%fused_computation.63 | convolution fusion | flops 9668395008 | bytes 33038336 | tf_op jit(solution)/vmap(jvp())/dot_general | solution.py:21
  116.1 14.8 %convolution_convert_fusion.1 = bf16[2048,3072]{1,0:T(8,128)(2,1)} fusion(bf16[2,3072,768]{2,1,0:T(8,128)(2,1)} %param.3, bf16[1,2048,768]{2,1,0:T(8,128)(2,1)S(1)} %copy-done.3), kind=kOutput, calls=%fused_computation.44 | convolution fusion | flops 9669967872 | bytes 20447232 | tf_op jit(solution)/vmap(transpose(jvp()))/dot_general | solution.py:9
  134.1 21.1 %fusion.6 = bf16[2048,3072]{1,0:T(8,128)(2,1)S(1)} fusion(f32[2048,3072]{1,0:T(8,128)} %fusion.42, f32[2048,3072]{1,0:T(8,128)} %fusion.46, bf16[2048,3072]{1,0:T(8,128)(2,1)} %convolution_convert_fusion.1), kind=kLoop, calls=%fused_computation.11 | loop fusion | flops 75497472 | bytes 75497472
  159.7 12.5 %fusion.69 = bf16[2048,768]{0,1:T(8,128)(2,1)S(1)} fusion(bf16[2048,3072]{1,0:T(8,128)(2,1)S(1)} %fusion.6, bf16[2,768,3072]{2,1,0:T(8,128)(2,1)} %param), kind=kOutput, calls=%fused_computation.87 | convolution fusion | flops 9663676416 | bytes 20447232 | tf_op jit(solution)/vmap(transpose(jvp()))/dot_general | solution.py:20
  172.2 17.5 %fusion.41 = (f32[2048]{0:T(1024)S(1)}, bf16[2048,768]{0,1:T(8,128)(2,1)S(1)}) fusion(bf16[1,2048,768]{1,2,0:T(8,128)(2,1)S(1)} %copy-done.7, bf16[2048,768]{0,1:T(8,128)(2,1)S(1)} %fusion.69, bf16[2,768,3072]{2,1,0:T(8,128)(2,1)} %param.5, bf16[2048,3072]{1,0:T(8,128)(2,1)} %convolution_convert_fusion.1, f32[2048,3072]{1,0:T(8,128)} %fusion.42), kind=kOutput, calls=%fused_computation.58 | convolution fusion | flops 9710860288 | bytes 51912704 | tf_op jit(solution)/vmap(transpose(jvp()))/dot_general | solution.py:21
  193.7 15.9 %fusion.131 = f32[768,3072]{0,1:T(8,128)} fusion(bf16[2048,768]{0,1:T(8,128)(2,1)S(1)} %fusion.79, bf16[2048,3072]{1,0:T(8,128)(2,1)} %fusion.26), kind=kOutput, calls=%fused_computation.151 | convolution fusion | flops 9663676416 | bytes 25165824 | tf_op jit(solution)/vmap(transpose(jvp()))/dot_general | solution.py:9
  211.5 23.8 %fusion.28 = f32[3072,768]{1,0:T(8,128)} fusion(f32[2048,3072]{1,0:T(8,128)} %fusion.46, f32[2048,3072]{1,0:T(8,128)} %fusion.42, bf16[1,2048,768]{2,1,0:T(8,128)(2,1)S(1)} %copy-done.4), kind=kOutput, calls=%fused_computation.37 | convolution fusion | flops 9701425152 | bytes 62914560 | tf_op jit(solution)/vmap(transpose(jvp()))/dot_general | solution.py:9
  235.5 16.0 %convolution_convert_fusion = bf16[2048,3072]{1,0:T(8,128)(2,1)} fusion(bf16[2048,768]{0,1:T(8,128)(2,1)} %copy-done.8, bf16[2,3072,768]{2,1,0:T(8,128)(2,1)} %param.3), kind=kOutput, calls=%fused_computation.43 | convolution fusion | flops 9669967872 | bytes 20447232 | tf_op jit(solution)/vmap(transpose(jvp()))/dot_general | solution.py:9
  251.5 20.8 %fusion.2 = f32[3072,768]{0,1:T(8,128)} fusion(bf16[2048,3072]{1,0:T(8,128)(2,1)} %convolution_convert_fusion, f32[2048,3072]{1,0:T(8,128)} %fusion.54, bf16[1,2048,768]{2,1,0:T(8,128)(2,1)S(1)} %copy-done.2, f32[2048]{0:T(1024)S(1)} %copy-done.17), kind=kOutput, calls=%fused_computation.8 | convolution fusion | flops 9706143744 | bytes 50339840 | tf_op jit(solution)/vmap(transpose(jvp()))/dot_general | solution.py:21
  272.9 21.6 %fusion.22 = f32[3072,768]{0,1:T(8,128)} fusion(bf16[2048,3072]{1,0:T(8,128)(2,1)} %convolution_convert_fusion.1, f32[2048,3072]{1,0:T(8,128)} %fusion.42, bf16[1,2048,768]{1,2,0:T(8,128)(2,1)} %copy-done.6, f32[2048]{0:T(1024)S(1)} %bitcast.337), kind=kOutput, calls=%fused_computation.33 | convolution fusion | flops 9706143744 | bytes 50339840 | tf_op jit(solution)/vmap(transpose(jvp()))/dot_general | solution.py:21
  294.6 16.0 %fusion.112 = f32[3072,768]{0,1:T(8,128)} fusion(bf16[2048,3072]{1,0:T(8,128)(2,1)} %copy-done, bf16[1,2048,768]{1,2,0:T(8,128)(2,1)} %copy-done.6, f32[2048]{0:T(1024)S(1)} %bitcast.338), kind=kOutput, calls=%fused_computation.127 | convolution fusion | flops 9668395008 | bytes 25174016 | tf_op jit(solution)/vmap(transpose(jvp()))/dot_general | solution.py:20
  310.7 28.1 %fusion.10 = f32[3072,768]{0,1:T(8,128)} fusion(f32[2048,3072]{1,0:T(8,128)} %fusion.54, f32[2048,3072]{1,0:T(8,128)} %fusion.52, bf16[2048,3072]{1,0:T(8,128)(2,1)} %convolution_convert_fusion, bf16[1,2048,768]{2,1,0:T(8,128)(2,1)S(1)} %copy-done.2, f32[2048]{0:T(1024)S(1)} %copy-done.17), kind=kOutput, calls=%fused_computation.15 | convolution fusion | flops 9737601024 | bytes 75505664 | tf_op jit(solution)/vmap(transpose(jvp()))/dot_general | solution.py:20
  358.3 64.2 %reduce-scatter.25.cloned.1.call-done = f32[3072,96]{0,1:T(8,128)} async-done(((f32[3072,768]{0,1:T(8,128)}), f32[3072,96]{0,1:T(8,128)}) %reduce-scatter.25.cloned.1.call-update) | async-done | bytes 1179664
  423.8 69.4 %reduce-scatter.23.cloned.1.call-done = f32[3072,96]{0,1:T(8,128)} async-done(((f32[3072,768]{0,1:T(8,128)}), f32[3072,96]{0,1:T(8,128)}) %reduce-scatter.23.cloned.1.call-update) | async-done | bytes 1179664
  500.5 64.0 %reduce-scatter.19.cloned.1.call-done = f32[3072,96]{0,1:T(8,128)} async-done(((f32[3072,768]{0,1:T(8,128)}), f32[3072,96]{0,1:T(8,128)}) %reduce-scatter.19.cloned.1.call-update) | async-done | bytes 1179664
  565.8 70.0 %reduce-scatter.21.cloned.1.call-done = f32[3072,96]{0,1:T(8,128)} async-done(((f32[3072,768]{0,1:T(8,128)}), f32[3072,96]{0,1:T(8,128)}) %reduce-scatter.21.cloned.1.call-update) | async-done | bytes 1179664
  643.0 47.6 %all-gather.14.cloned.1.call-done = bf16[1,2,3072,768]{3,2,1,0:T(8,128)(2,1)} async-done(((bf16[1,2,384,768]{3,2,1,0:T(8,128)(2,1)}), bf16[1,2,3072,768]{3,2,1,0:T(8,128)(2,1)}) %all-gather.14.cloned.1.call-update) | async-done | bytes 9437200 | tf_op jit(solution)/reshape | solution.py:52
  690.6 55.4 %all-gather.12.cloned.1.call-done = bf16[1,2,768,3072]{3,2,1,0:T(8,128)(2,1)} async-done(((bf16[1,2,96,3072]{3,2,1,0:T(8,128)(2,1)}), bf16[1,2,768,3072]{3,2,1,0:T(8,128)(2,1)}) %all-gather.12.cloned.1.call-update) | async-done | bytes 9437200 | tf_op jit(solution)/reshape | solution.py:52
  746.0 55.4 %all-gather.10.cloned.1.call-done = bf16[1,2,768,3072]{3,2,1,0:T(8,128)(2,1)} async-done(((bf16[1,2,96,3072]{3,2,1,0:T(8,128)(2,1)}), bf16[1,2,768,3072]{3,2,1,0:T(8,128)(2,1)}) %all-gather.10.cloned.1.call-update) | async-done | bytes 9437200 | tf_op jit(solution)/reshape | solution.py:52
  (76 shorter events, 83.6 us)
Async XLA Ops:
  7.2 7.4 copy-start.1
  7.2 331.7 %reduce-scatter.29.cloned.1.call-start = ((), (), s32[]{:S(2)}) async-start(), calls=%async_computation.14 | async-start | bytes 10616832
  14.6 16.0 %copy-start.16 = (f32[2048]{0:T(1024)}, f32[2048]{0:T(1024)S(1)}, u32[]{:S(2)}) copy-start(f32[2048]{0:T(1024)S(1)} %add_rsqrt_fusion) | copy-start | bytes 24580
  46.5 21.8 %copy-start.5 = (bf16[1,2048,768]{1,2,0:T(8,128)(2,1)S(1)}, bf16[1,2048,768]{1,2,0:T(8,128)(2,1)}, u32[]{:S(2)}) copy-start(bf16[1,2048,768]{1,2,0:T(8,128)(2,1)} %copy) | copy-start | bytes 9437188
  83.3 16.8 %copy-start.6 = (bf16[1,2048,768]{1,2,0:T(8,128)(2,1)}, bf16[1,2048,768]{1,2,0:T(8,128)(2,1)S(1)}, u32[]{:S(2)}) copy-start(bf16[1,2048,768]{1,2,0:T(8,128)(2,1)S(1)} %get-tuple-element.10) | copy-start | bytes 9437188
  84.0 105.8 %copy-start.14 = (f32[1,2048]{1,0:T(1,128)}, f32[1,2048]{1,0:T(1,128)S(1)}, u32[]{:S(2)}) copy-start(f32[1,2048]{1,0:T(1,128)S(1)} %rsqrt.29) | copy-start | bytes 24580
  100.1 16.0 %copy-start.3 = (bf16[1,2048,768]{2,1,0:T(8,128)(2,1)S(1)}, bf16[1,2048,768]{2,1,0:T(8,128)(2,1)}, u32[]{:S(2)}) copy-start(bf16[1,2048,768]{2,1,0:T(8,128)(2,1)} %param.2) | copy-start | bytes 9437188
  155.2 4.5 copy-start
  159.7 12.5 %copy-start.7 = (bf16[1,2048,768]{1,2,0:T(8,128)(2,1)S(1)}, bf16[1,2048,768]{1,2,0:T(8,128)(2,1)}, u32[]{:S(2)}) copy-start(bf16[1,2048,768]{1,2,0:T(8,128)(2,1)} %copy-done.6) | copy-start | bytes 9437188
  172.2 17.5 %copy-start.13 = (f32[2048]{0:T(1024)S(1)}, f32[2048]{0:T(1024)}, u32[]{:S(2)}) copy-start(f32[2048]{0:T(1024)} %copy-done.12) | copy-start | bytes 24580
  209.7 1.9 copy-start.4
  209.7 141.3 %reduce-scatter.27.cloned.1.call-start = ((), (), s32[]{:S(2)}) async-start(), calls=%async_computation.13 | async-start | bytes 10616832
  235.4 16.1 %copy-start.2 = (bf16[1,2048,768]{2,1,0:T(8,128)(2,1)S(1)}, bf16[1,2048,768]{2,1,0:T(8,128)(2,1)}, u32[]{:S(2)}) copy-start(bf16[1,2048,768]{2,1,0:T(8,128)(2,1)} %param.4) | copy-start | bytes 9437188
  235.4 16.1 %copy-start.17 = (f32[2048]{0:T(1024)S(1)}, f32[2048]{0:T(1024)}, u32[]{:S(2)}) copy-start(f32[2048]{0:T(1024)} %copy-done.16) | copy-start | bytes 24580
  235.4 187.1 %reduce-scatter.25.cloned.1.call-start = ((), (), s32[]{:S(2)}) async-start(), calls=%async_computation.12 | async-start | bytes 10616832
  272.3 220.9 %reduce-scatter.23.cloned.1.call-start = ((), (), s32[]{:S(2)}) async-start(), calls=%async_computation.11 | async-start | bytes 10616832
  294.5 270.0 %reduce-scatter.19.cloned.1.call-start = ((), (), s32[]{:S(2)}) async-start(), calls=%async_computation.9 | async-start | bytes 10616832
  310.6 325.2 %reduce-scatter.21.cloned.1.call-start = ((), (), s32[]{:S(2)}) async-start(), calls=%async_computation.10 | async-start | bytes 10616832
  338.8 13.5 %copy-start.9 = (f32[2,384,768]{2,1,0:T(8,128)S(1)}, f32[2,384,768]{2,1,0:T(8,128)}, u32[]{:S(2)}) copy-start(f32[2,384,768]{2,1,0:T(8,128)} %param.10) | copy-start | bytes 7077892
  338.8 351.8 %all-gather.14.cloned.1.call-start = ((), (), s32[]{:S(2)}) async-start(), calls=%async_computation.8 | async-start | bytes 10616832 | tf_op jit(solution)/reshape | solution.py:52
  358.2 136.3 %copy-start.10 = (f32[2,96,3072]{2,1,0:T(8,128)S(1)}, f32[2,96,3072]{2,1,0:T(8,128)}, u32[]{:S(2)}) copy-start(f32[2,96,3072]{2,1,0:T(8,128)} %param.8) | copy-start | bytes 7077892
  358.2 387.8 %all-gather.12.cloned.1.call-start = ((), (), s32[]{:S(2)}) async-start(), calls=%async_computation.7 | async-start | bytes 10616832 | tf_op jit(solution)/reshape | solution.py:52
  500.4 136.8 %copy-start.11 = (f32[2,96,3072]{2,1,0:T(8,128)S(1)}, f32[2,96,3072]{2,1,0:T(8,128)}, u32[]{:S(2)}) copy-start(f32[2,96,3072]{2,1,0:T(8,128)} %param.6) | copy-start | bytes 7077892
  500.4 301.0 %all-gather.10.cloned.1.call-start = ((), (), s32[]{:S(2)}) async-start(), calls=%async_computation.6 | async-start | bytes 10616832 | tf_op jit(solution)/reshape | solution.py:52
  (3 other events, 3.0 us)
Sparse Core Ops, SparseCore 0:
  209.8 70.2 reduce-scatter.28
  283.5 67.4 reduce-scatter.26
  355.0 67.4 reduce-scatter.24
  425.8 67.4 reduce-scatter.22
  497.1 67.4 reduce-scatter.18
  568.4 67.4 reduce-scatter.20
  637.6 52.9 all-gather.13
  693.0 52.9 all-gather.11
  748.4 52.9 all-gather.9
where the time goes:
time: 842 us; the launch traced here: 833 us
  waiting for transfers between devices  437 us (52%)
  matrix products  266 us (32%)
  other arithmetic  73.6 us (9%)
  local copies, waits for them, and re-layouts  41.8 us (5%)
  between operations  14.6 us (2%)
    unnamed x15, waiting for transfers between devices  278 us
    reshape x3, waiting for transfers between devices, step(): t.reshape(-1, *t.shape[2:])  158 us
    dot_general x5, matrix products, layer(): up = jnp.dot(a, w['w_up'], preferred_element_type=jnp.float32)  91.7 us
    dot_general x5, matrix products, layer(): gate = jnp.dot(a, w['w_gate'], preferred_element_type=jnp.float32)  88.7 us
    dot_general x5, matrix products, matmul(): jnp.dot(a, w, preferred_element_type=jnp.float32).astype(jnp.bfloat16)  85.6 us
    unnamed x3, other arithmetic  45.1 us
    unnamed x41, local copies, waits for them, and re-layouts  41.7 us
    reshape x3, other arithmetic, step(): t.reshape(-1, *t.shape[2:])  17.5 us
  transfers between devices with their start and end apart: 9, of which 8 were waited for; matrix products, arithmetic and copies ran while one was open for 18% of the time, Pallas kernels for 0%

commit v1 on v0

v1 whole, which is shorter than its diff:
```python
import jax
import jax.numpy as jnp
from jax import lax
from jax.sharding import PartitionSpec as P

NAMES = ("w_gate", "w_up", "w_down")


def matmul(a, w):
    return jnp.dot(a, w, preferred_element_type=jnp.float32).astype(jnp.bfloat16)


def normed(h):
    wide = h.astype(jnp.float32)
    scale = lax.rsqrt(jnp.mean(wide**2, -1, keepdims=True) + 1e-6)
    return (wide * scale).astype(jnp.bfloat16)


def layer(h, wg, wu, wd):
    a = normed(h)
    gate = jnp.dot(a, wg, preferred_element_type=jnp.float32)
    up = jnp.dot(a, wu, preferred_element_type=jnp.float32)
    return h + matmul((jax.nn.silu(gate) * up).astype(jnp.bfloat16), wd)


def adamw(w, m, v, g):
    m = 0.9 * m + 0.1 * g
    v = 0.95 * v + 0.05 * g * g
    step = m * lax.rsqrt(v + 1e-8) + 0.1 * w
    return (w - 0.02 * step).astype(jnp.bfloat16), m, v


def solution(mesh):
    def body(x, dy, wg, wu, wd, mg, mu, md, vg, vu, vd):
        me = lax.axis_index("dp")
        n = lax.axis_size("dp")

        def f(ws):
            h = x[0]
            for l in range(2):
                h = layer(h, *ws[l])
            return h

        ws = [tuple(w[l] for w in (wg, wu, wd)) for l in range(2)]
        _, back = jax.vjp(f, ws)
        grads = back(dy[0])[0]
        new = [[], [], []]
        ms, vs = [[], [], []], [[], [], []]
        for l in (1, 0):
            for i in (2, 0, 1):
                w, m, v = (wg, wu, wd)[i][l], (mg, mu, md)[i][l], (vg, vu, vd)[i][l]
                g = lax.psum_scatter(grads[l][i], "dp", scatter_dimension=0, tiled=True).astype(jnp.float32)
                rows = w.shape[0] // n
                own = lax.dynamic_slice_in_dim(w, me * rows, rows, 0).astype(jnp.float32)
                nw, nm, nv = adamw(own, m, v, g)
                new[i].append(lax.all_gather(nw, "dp", axis=0, tiled=True))
                ms[i].append(nm)
                vs[i].append(nv)
        return tuple(jnp.stack(t[i][::-1]) for t in (new, ms, vs) for i in range(3))

    tok, whole, rows = P(("rep", "dp")), P(), P(None, "dp")
    return jax.shard_map(
        body,
        mesh=mesh,
        in_specs=(tok, tok) + (whole,) * 3 + (rows,) * 6,
        out_specs=(P("rep"),) * 3 + (P("rep", "dp"),) * 6,
        check_vma=False,
    )
```

time: 842 us -> 696 us (0.83)
  waiting for transfers between devices: 437 us -> 284 us
  matrix products: 266 us -> 299 us
  other arithmetic: 73.6 us -> 55.6 us
    unnamed x15 -> x12, waiting for transfers between devices: 278 us -> 1.9 us
    all_gather x0 -> x6, waiting for transfers between devices: none -> 174 us  [body(): new[i].append(lax.all_gather(nw, 'dp', axis=0, tiled=True))]
    reshape x3 -> x0, waiting for transfers between devices: 158 us -> none  [step(): t.reshape(-1, *t.shape[2:])]
    reduce_scatter x0 -> x6, waiting for transfers between devices: none -> 108 us  [body(): lax.psum_scatter(grads[l][i], 'dp', scatter_dimension=0, tiled=True)]
    unnamed x3 -> x0, other arithmetic: 45.1 us -> none
    another operation x0 -> x6, other arithmetic: none -> 34.7 us  [body(): jnp.stack(t[i][::-1])]
    dot_general x10, matrix products: 180 us -> 215 us  [the longest x5 115 us: layer(): gate = jnp.dot(a, wg, preferred_element_type=jnp.float32)]
    unnamed x41 -> x42, local copies, waits for them, and re-layouts: 41.7 us -> 11 us
  transfers between devices with their start and end apart: 9 -> 12, of which waited for: 8 -> 9; matrix products, arithmetic and copies ran while one was open for 18% -> 32% of each run, Pallas kernels for 0% -> 0%
where the time goes in v1:
time: 696 us; the launch traced here: 689 us
  matrix products  299 us (43%)
  waiting for transfers between devices  284 us (41%)
  other arithmetic  55.6 us (8%)
  local copies, waits for them, and re-layouts  35.7 us (5%)
  between operations  14.6 us (2%)
    all_gather x6, waiting for transfers between devices, body(): new[i].append(lax.all_gather(nw, 'dp', axis=0, tiled=True))  174 us
    dot_general x5, matrix products, layer(): gate = jnp.dot(a, wg, preferred_element_type=jnp.float32)  115 us
    reduce_scatter x6, waiting for transfers between devices, body(): lax.psum_scatter(grads[l][i], 'dp', scatter_dimension=0, tiled=True)  108 us
    dot_general x5, matrix products, layer(): up = jnp.dot(a, wu, preferred_element_type=jnp.float32)  99.4 us
    dot_general x5, matrix products, matmul(): jnp.dot(a, w, preferred_element_type=jnp.float32).astype(jnp.bfloat16)  84.4 us
    another operation x6, other arithmetic, body(): jnp.stack(t[i][::-1])  34.7 us
    convert_element_type x3, other arithmetic, adamw(): return ((w - 0.02 * step).astype(jnp.bfloat16), m, v)  18 us
    slice x2, local copies, waits for them, and re-layouts, body(): ws = [tuple((w[l] for w in (wg, wu, wd))) for l in range(2)]  16.3 us
  transfers between devices with their start and end apart: 12, of which 9 were waited for; matrix products, arithmetic and copies ran while one was open for 32% of the time, Pallas kernels for 0%

profile of v1, /device:TPU:0, one launch (start us, length us, event | category | flops | bytes accessed | tf_op | source)
XLA Modules:
  0.0 689.4 jit_solution(7782368054916292468)
XLA Ops:
  11.1 18.0 %fusion.41 = f32[2048,3072]{1,0:T(8,128)} fusion(bf16[1,2048,768]{2,1,0:T(8,128)(2,1)} %param.11, f32[2048]{0:T(1024)S(1)} %add_rsqrt_fusion, bf16[2,768,3072]{2,1,0:T(8,128)(2,1)} %param.13), kind=kOutput, calls=%fused_computation.63 | convolution fusion | flops 9668395008 | bytes 33038336 | tf_op jit(solution)/shard_map/jvp()/dot_general | solution.py:21
  29.1 27.6 %multiply_convert_fusion.1 = (bf16[2048,3072]{1,0:T(8,128)(2,1)}, f32[2048,3072]{1,0:T(8,128)}) fusion(f32[2048,3072]{1,0:T(8,128)} %fusion.41, bf16[2,768,3072]{2,1,0:T(8,128)(2,1)} %param.14, bf16[1,2048,768]{2,1,0:T(8,128)(2,1)} %param.11, f32[2048]{0:T(1024)S(1)} %add_rsqrt_fusion), kind=kOutput, calls=%fused_computation.17 | convolution fusion | flops 9706143744 | bytes 70787072 | tf_op jit(solution)/shard_map/jvp()/dot_general | solution.py:22
  56.7 16.3 %fusion.19 = (f32[2048]{0:T(1024)S(1)}, bf16[2048,768]{0,1:T(8,128)(2,1)}) fusion(bf16[2048,3072]{1,0:T(8,128)(2,1)} %get-tuple-element.33, bf16[2,3072,768]{2,1,0:T(8,128)(2,1)} %param.15, bf16[1,2048,768]{1,2,0:T(8,128)(2,1)S(1)} %copy.20), kind=kOutput, calls=%fused_computation.40 | convolution fusion | flops 9671538688 | bytes 23601152 | tf_op jit(solution)/shard_map/jvp()/dot_general | solution.py:10
  73.1 15.0 %convolution_convert_fusion.1 = bf16[2048,3072]{1,0:T(8,128)(2,1)} fusion(bf16[1,2048,768]{2,1,0:T(8,128)(2,1)S(1)} %copy-done.10, bf16[2,3072,768]{2,1,0:T(8,128)(2,1)} %param.15), kind=kOutput, calls=%fused_computation.25 | convolution fusion | flops 9669967872 | bytes 20447232 | tf_op jit(solution)/shard_map/transpose(jvp())/dot_general | solution.py:10
  88.0 15.9 %fusion.28 = f32[2048,3072]{1,0:T(8,128)} fusion(bf16[2048,768]{0,1:T(8,128)(2,1)S(1)} %copy-done.12, f32[2048]{0:T(1024)S(1)} %fusion.112, bf16[2,768,3072]{2,1,0:T(8,128)(2,1)} %param.14), kind=kOutput, calls=%fused_computation.50 | convolution fusion | flops 9668395008 | bytes 33038336 | tf_op jit(solution)/shard_map/jvp()/dot_general | solution.py:22
  103.9 39.5 %fusion.2 = (bf16[2048,3072]{1,0:T(8,128)(2,1)}, f32[2048,3072]{1,0:T(8,128)}) fusion(f32[2048,3072]{1,0:T(8,128)} %fusion.28, bf16[2048,3072]{1,0:T(8,128)(2,1)} %convolution_convert_fusion.1, bf16[2,768,3072]{2,1,0:T(8,128)(2,1)} %param.13, bf16[2048,768]{0,1:T(8,128)(2,1)} %get-tuple-element.36, f32[2048]{0:T(1024)S(1)} %fusion.112), kind=kOutput, calls=%fused_computation.8 | convolution fusion | flops 9743892480 | bytes 83369984 | tf_op jit(solution)/shard_map/jvp()/dot_general | solution.py:21
  143.5 22.4 %fusion.22 = bf16[3072,768]{1,0:T(8,128)(2,1)} fusion(f32[2048,3072]{1,0:T(8,128)} %fusion.28, bf16[1,2048,768]{2,1,0:T(8,128)(2,1)S(1)} %copy-done.11, f32[2048,3072]{1,0:T(8,128)} %get-tuple-element.38), kind=kOutput, calls=%fused_computation.44 | convolution fusion | flops 9703784448 | bytes 58195968 | tf_op jit(solution)/shard_map/transpose(jvp())/dot_general | solution.py:10
  165.9 19.1 %fusion.44 = bf16[2048,768]{0,1:T(8,128)(2,1)} fusion(bf16[2048,3072]{1,0:T(8,128)(2,1)} %convolution_convert_fusion.1, bf16[2,768,3072]{2,1,0:T(8,128)(2,1)} %param.14, f32[2048,3072]{1,0:T(8,128)} %get-tuple-element.38), kind=kOutput, calls=%fused_computation.65 | convolution fusion | flops 9702998016 | bytes 45613056 | tf_op jit(solution)/shard_map/transpose(jvp())/dot_general | solution.py:22
  188.2 16.2 %fusion.21 = (f32[2048]{0:T(1024)S(1)}, bf16[2048,768]{0,1:T(8,128)(2,1)S(1)}) fusion(bf16[2048,768]{0,1:T(8,128)(2,1)} %get-tuple-element.36, bf16[2048,768]{0,1:T(8,128)(2,1)} %fusion.44, bf16[2048,3072]{1,0:T(8,128)(2,1)} %get-tuple-element.37, bf16[2,768,3072]{2,1,0:T(8,128)(2,1)} %param.13), kind=kOutput, calls=%fused_computation.42 | convolution fusion | flops 9671538688 | bytes 26746880 | tf_op jit(solution)/shard_map/transpose(jvp())/dot_general | solution.py:21
  208.3 14.7 %convolution_convert_fusion.2 = bf16[3072,768]{1,0:T(8,128)(2,1)} fusion(bf16[2048,3072]{1,0:T(8,128)(2,1)} %get-tuple-element.33, bf16[2048,768]{0,1:T(8,128)(2,1)S(1)} %fusion.54), kind=kOutput, calls=%fused_computation.48 | convolution fusion | flops 9666035712 | bytes 20447232 | tf_op jit(solution)/shard_map/transpose(jvp())/dot_general | solution.py:10
  224.9 18.5 %fusion.23 = bf16[768,3072]{1,0:T(8,128)(2,1)} fusion(bf16[2048,3072]{1,0:T(8,128)(2,1)} %convolution_convert_fusion.1, bf16[2048,768]{0,1:T(8,128)(2,1)S(1)} %copy-done.14, f32[2048]{0:T(1024)S(1)} %fusion.112, f32[2048,3072]{1,0:T(8,128)} %get-tuple-element.38), kind=kOutput, calls=%fused_computation.45 | convolution fusion | flops 9708503040 | bytes 45621248 | tf_op jit(solution)/shard_map/transpose(jvp())/dot_general | solution.py:22
  243.6 16.0 %convolution_convert_fusion = bf16[2048,3072]{1,0:T(8,128)(2,1)} fusion(bf16[2048,768]{0,1:T(8,128)(2,1)} %copy-done.15, bf16[2,3072,768]{2,1,0:T(8,128)(2,1)} %param.15), kind=kOutput, calls=%fused_computation.24 | convolution fusion | flops 9669967872 | bytes 20447232 | tf_op jit(solution)/shard_map/transpose(jvp())/dot_general | solution.py:10
  259.6 18.4 %fusion.27 = bf16[768,3072]{1,0:T(8,128)(2,1)} fusion(bf16[2048,3072]{1,0:T(8,128)(2,1)} %convolution_convert_fusion, f32[2048,3072]{1,0:T(8,128)} %fusion.41, bf16[1,2048,768]{1,2,0:T(8,128)(2,1)S(1)} %copy-done.1, f32[2048]{0:T(1024)S(1)} %copy-done.19), kind=kOutput, calls=%fused_computation.47 | convolution fusion | flops 9708503040 | bytes 45621248 | tf_op jit(solution)/shard_map/transpose(jvp())/dot_general | solution.py:22
  278.0 15.7 %convolution_convert_fusion.3 = bf16[768,3072]{1,0:T(8,128)(2,1)} fusion(bf16[2048,3072]{1,0:T(8,128)(2,1)} %get-tuple-element.37, bf16[2048,768]{0,1:T(8,128)(2,1)} %get-tuple-element.36, f32[2048]{0:T(1024)S(1)} %fusion.112), kind=kOutput, calls=%fused_computation.49 | convolution fusion | flops 9668395008 | bytes 20455424 | tf_op jit(solution)/shard_map/transpose(jvp())/dot_general | solution.py:21
  293.8 25.8 %fusion.24 = bf16[768,3072]{1,0:T(8,128)(2,1)} fusion(f32[2048,3072]{1,0:T(8,128)} %fusion.41, f32[2048,3072]{1,0:T(8,128)} %get-tuple-element.34, bf16[2048,3072]{1,0:T(8,128)(2,1)} %convolution_convert_fusion, bf16[1,2048,768]{1,2,0:T(8,128)(2,1)S(1)} %copy-done.1, f32[2048]{0:T(1024)S(1)} %copy-done.19), kind=kOutput, calls=%fused_computation.46 | convolution fusion | flops 9739960320 | bytes 70787072 | tf_op jit(solution)/shard_map/transpose(jvp())/dot_general | solution.py:21
  342.3 26.1 %reduce-scatter.11.cloned.1.call-done = bf16[96,3072]{1,0:T(8,128)(2,1)} async-done(((bf16[768,3072]{1,0:T(8,128)(2,1)}), bf16[96,3072]{1,0:T(8,128)(2,1)}) %reduce-scatter.11.cloned.1.call-update) | async-done | bytes 589840 | tf_op jit(solution)/shard_map/reduce_scatter | solution.py:52
  383.8 32.8 %reduce-scatter.9.cloned.1.call-done = bf16[96,3072]{1,0:T(8,128)(2,1)} async-done(((bf16[768,3072]{1,0:T(8,128)(2,1)}), bf16[96,3072]{1,0:T(8,128)(2,1)}) %reduce-scatter.9.cloned.1.call-update) | async-done | bytes 589840 | tf_op jit(solution)/shard_map/reduce_scatter | solution.py:52
  416.6 48.9 %reduce-scatter.7.cloned.1.call-done = bf16[96,3072]{1,0:T(8,128)(2,1)} async-done(((bf16[768,3072]{1,0:T(8,128)(2,1)}), bf16[96,3072]{1,0:T(8,128)(2,1)}) %reduce-scatter.7.cloned.1.call-update) | async-done | bytes 589840 | tf_op jit(solution)/shard_map/reduce_scatter | solution.py:52
  483.1 17.2 %all-gather.15.cloned.1.call-done = bf16[3072,768]{1,0:T(8,128)(2,1)} async-done(((bf16[384,768]{1,0:T(8,128)(2,1)}), bf16[3072,768]{1,0:T(8,128)(2,1)}) %all-gather.15.cloned.1.call-update) | async-done | bytes 4718608 | tf_op jit(solution)/shard_map/all_gather | solution.py:56
  500.3 34.8 %all-gather.17.cloned.1.call-done = bf16[3072,768]{1,0:T(8,128)(2,1)} async-done(((bf16[384,768]{1,0:T(8,128)(2,1)}), bf16[3072,768]{1,0:T(8,128)(2,1)}) %all-gather.17.cloned.1.call-update) | async-done | bytes 4718608 | tf_op jit(solution)/shard_map/all_gather | solution.py:56
  543.5 26.4 %all-gather.11.cloned.1.call-done = bf16[768,3072]{1,0:T(8,128)(2,1)} async-done(((bf16[96,3072]{1,0:T(8,128)(2,1)}), bf16[768,3072]{1,0:T(8,128)(2,1)}) %all-gather.11.cloned.1.call-update) | async-done | bytes 4718608 | tf_op jit(solution)/shard_map/all_gather | solution.py:56
  569.9 34.6 %all-gather.13.cloned.1.call-done = bf16[768,3072]{1,0:T(8,128)(2,1)} async-done(((bf16[96,3072]{1,0:T(8,128)(2,1)}), bf16[768,3072]{1,0:T(8,128)(2,1)}) %all-gather.13.cloned.1.call-update) | async-done | bytes 4718608 | tf_op jit(solution)/shard_map/all_gather | solution.py:56
  612.9 26.4 %all-gather.7.cloned.1.call-done = bf16[768,3072]{1,0:T(8,128)(2,1)} async-done(((bf16[96,3072]{1,0:T(8,128)(2,1)}), bf16[768,3072]{1,0:T(8,128)(2,1)}) %all-gather.7.cloned.1.call-update) | async-done | bytes 4718608 | tf_op jit(solution)/shard_map/all_gather | solution.py:56
  639.3 34.6 %all-gather.9.cloned.1.call-done = bf16[768,3072]{1,0:T(8,128)(2,1)} async-done(((bf16[96,3072]{1,0:T(8,128)(2,1)}), bf16[768,3072]{1,0:T(8,128)(2,1)}) %all-gather.9.cloned.1.call-update) | async-done | bytes 4718608 | tf_op jit(solution)/shard_map/all_gather | solution.py:56
  (86 shorter events, 93.8 us)
Async XLA Ops:
  7.2 320.4 %reduce-scatter.17.cloned.1.call-start = ((), (), s32[]{:S(2)}) async-start(), calls=%async_computation.16 | async-start | bytes 5308416 | tf_op jit(solution)/shard_map/reduce_scatter | solution.py:52
  10.4 46.3 %copy-start = (bf16[1,2048,768]{1,2,0:T(8,128)(2,1)}, bf16[1,2048,768]{1,2,0:T(8,128)(2,1)S(1)}, u32[]{:S(2)}) copy-start(bf16[1,2048,768]{1,2,0:T(8,128)(2,1)S(1)} %copy.20) | copy-start | bytes 9437188
  11.1 18.0 %copy-start.18 = (f32[2048]{0:T(1024)}, f32[2048]{0:T(1024)S(1)}, u32[]{:S(2)}) copy-start(f32[2048]{0:T(1024)S(1)} %add_rsqrt_fusion) | copy-start | bytes 24580
  56.7 16.3 %copy-start.10 = (bf16[1,2048,768]{2,1,0:T(8,128)(2,1)S(1)}, bf16[1,2048,768]{2,1,0:T(8,128)(2,1)}, u32[]{:S(2)}) copy-start(bf16[1,2048,768]{2,1,0:T(8,128)(2,1)} %param.12) | copy-start | bytes 9437188
  73.0 15.0 %copy-start.16 = (f32[2048]{0:T(1024)}, f32[2048]{0:T(1024)S(1)}, u32[]{:S(2)}) copy-start(f32[2048]{0:T(1024)S(1)} %get-tuple-element.35) | copy-start | bytes 24580
  73.0 15.0 %copy-start.12 = (bf16[2048,768]{0,1:T(8,128)(2,1)S(1)}, bf16[2048,768]{0,1:T(8,128)(2,1)}, u32[]{:S(2)}) copy-start(bf16[2048,768]{0,1:T(8,128)(2,1)} %get-tuple-element.36) | copy-start | bytes 9437188
  103.9 39.5 %copy-start.11 = (bf16[1,2048,768]{2,1,0:T(8,128)(2,1)S(1)}, bf16[1,2048,768]{2,1,0:T(8,128)(2,1)}, u32[]{:S(2)}) copy-start(bf16[1,2048,768]{2,1,0:T(8,128)(2,1)} %param.12) | copy-start | bytes 9437188
  165.9 161.7 %reduce-scatter.15.cloned.1.call-start = ((), (), s32[]{:S(2)}) async-start(), calls=%async_computation.14 | async-start | bytes 5308416 | tf_op jit(solution)/shard_map/reduce_scatter | solution.py:52
  188.2 16.2 %copy-start.17 = (f32[2048]{0:T(1024)S(1)}, f32[2048]{0:T(1024)}, u32[]{:S(2)}) copy-start(f32[2048]{0:T(1024)} %copy-done.16) | copy-start | bytes 24580
  188.2 16.2 %copy-start.13 = (bf16[2048,768]{0,1:T(8,128)(2,1)S(1)}, bf16[2048,768]{0,1:T(8,128)(2,1)}, u32[]{:S(2)}) copy-start(bf16[2048,768]{0,1:T(8,128)(2,1)} %get-tuple-element.36) | copy-start | bytes 9437188
  223.1 119.2 %reduce-scatter.13.cloned.1.call-start = ((), (), s32[]{:S(2)}) async-start(), calls=%async_computation.12 | async-start | bytes 5308416 | tf_op jit(solution)/shard_map/reduce_scatter | solution.py:52
  243.5 16.1 %copy-start.1 = (bf16[1,2048,768]{1,2,0:T(8,128)(2,1)S(1)}, bf16[1,2048,768]{1,2,0:T(8,128)(2,1)}, u32[]{:S(2)}) copy-start(bf16[1,2048,768]{1,2,0:T(8,128)(2,1)} %copy-done) | copy-start | bytes 9437188
  243.5 16.1 %copy-start.19 = (f32[2048]{0:T(1024)S(1)}, f32[2048]{0:T(1024)}, u32[]{:S(2)}) copy-start(f32[2048]{0:T(1024)} %copy-done.18) | copy-start | bytes 24580
  243.5 124.8 %reduce-scatter.11.cloned.1.call-start = ((), (), s32[]{:S(2)}) async-start(), calls=%async_computation.10 | async-start | bytes 5308416 | tf_op jit(solution)/shard_map/reduce_scatter | solution.py:52
  278.0 138.7 %reduce-scatter.9.cloned.1.call-start = ((), (), s32[]{:S(2)}) async-start(), calls=%async_computation.8 | async-start | bytes 5308416 | tf_op jit(solution)/shard_map/reduce_scatter | solution.py:52
  293.7 171.8 %reduce-scatter.7.cloned.1.call-start = ((), (), s32[]{:S(2)}) async-start(), calls=%async_computation.6 | async-start | bytes 5308416 | tf_op jit(solution)/shard_map/reduce_scatter | solution.py:52
  319.6 180.7 %all-gather.15.cloned.1.call-start = ((), (), s32[]{:S(2)}) async-start(), calls=%async_computation.15 | async-start | bytes 5308416 | tf_op jit(solution)/shard_map/all_gather | solution.py:56
  333.1 202.0 %all-gather.17.cloned.1.call-start = ((), (), s32[]{:S(2)}) async-start(), calls=%async_computation.17 | async-start | bytes 5308416 | tf_op jit(solution)/shard_map/all_gather | solution.py:56
  333.9 236.0 %all-gather.11.cloned.1.call-start = ((), (), s32[]{:S(2)}) async-start(), calls=%async_computation.11 | async-start | bytes 5308416 | tf_op jit(solution)/shard_map/all_gather | solution.py:56
  374.6 229.9 %all-gather.13.cloned.1.call-start = ((), (), s32[]{:S(2)}) async-start(), calls=%async_computation.13 | async-start | bytes 5308416 | tf_op jit(solution)/shard_map/all_gather | solution.py:56
  375.2 264.1 %all-gather.7.cloned.1.call-start = ((), (), s32[]{:S(2)}) async-start(), calls=%async_computation.7 | async-start | bytes 5308416 | tf_op jit(solution)/shard_map/all_gather | solution.py:56
  471.7 202.2 %all-gather.9.cloned.1.call-start = ((), (), s32[]{:S(2)}) async-start(), calls=%async_computation.9 | async-start | bytes 5308416 | tf_op jit(solution)/shard_map/all_gather | solution.py:56
  472.3 4.0 copy-start.2
  476.3 4.0 copy-start.9
  (8 other events, 24.5 us)
Sparse Core Ops, SparseCore 0:
  166.0 47.8 reduce-scatter.16
  223.2 47.8 reduce-scatter.14
  274.4 45.0 reduce-scatter.12
  323.3 45.0 reduce-scatter.10
  371.6 45.0 reduce-scatter.8
  420.4 45.0 reduce-scatter.6
  467.3 32.9 all-gather.14
  502.1 32.9 all-gather.16
  536.9 32.9 all-gather.10
  571.5 32.9 all-gather.12
  606.3 32.9 all-gather.6
  641.0 32.9 all-gather.8

commit v2 on v1

v2 whole, which is shorter than its diff:
```python
import jax
import jax.numpy as jnp
from jax import lax
from jax.experimental import pallas as pl
from jax.experimental.pallas import tpu as pltpu
from jax.sharding import PartitionSpec as P

T, D, FF = 2048, 768, 3072
S = 512
B = 512
R = 192
NS = 6
LAG = 2
UNITS = 18
VMEM_LIMIT = 66_500_000
BF, F32 = jnp.bfloat16, jnp.float32


def nn(a, b):
    return jnp.dot(a, b, preferred_element_type=F32)


def nt(a, b):
    return lax.dot_general(a, b, (((1,), (1,)), ((), ())), preferred_element_type=F32)


def scale_of(wide):
    return lax.rsqrt(jnp.mean(wide * wide, -1, keepdims=True) + 1e-6)


def forward_kernel(x_ref, wg_ref, wu_ref, wd_ref, out_ref, a_ref, acc_ref):
    t = pl.program_id(0)

    def rows(i):
        return pl.ds(pl.multiple_of(i * B, B), B)

    @pl.when(t == 0)
    def _():
        @pl.loop(0, T // B)
        def _(i):
            wide = x_ref[rows(i), :].astype(F32)
            a_ref[rows(i), :] = (wide * scale_of(wide)).astype(BF)
            acc_ref[rows(i), :] = jnp.zeros((B, D), F32)

    @pl.loop(0, T // B)
    def _(i):
        a = a_ref[rows(i), :]
        gate = nn(a, wg_ref[0])
        up = nn(a, wu_ref[0])
        act = (gate * jax.nn.sigmoid(gate) * up).astype(BF)
        acc_ref[rows(i), :] += nn(act, wd_ref[0])

    @pl.when(t == pl.num_programs(0) - 1)
    def _():
        @pl.loop(0, T // B)
        def _(i):
            out_ref[rows(i), :] = x_ref[rows(i), :] + acc_ref[rows(i), :].astype(BF)


def forward(x, wg, wu, wd):
    whole = pl.BlockSpec((T, D), lambda t: (0, 0))
    cols = pl.BlockSpec((1, D, S), lambda t: (0, 0, t))
    return pl.pallas_call(
        forward_kernel,
        grid=(FF // S,),
        out_shape=jax.ShapeDtypeStruct((T, D), BF),
        in_specs=[whole, cols, cols, pl.BlockSpec((1, S, D), lambda t: (0, t, 0))],
        out_specs=whole,
        scratch_shapes=[pltpu.VMEM((T, D), BF), pltpu.VMEM((T, D), F32)],
        compiler_params=pltpu.CompilerParams(vmem_limit_bytes=56_000_000),
        name="forward0",
    )(x, wg, wu, wd)


S0, S1X, S1Y, S2X, S2Y, G1X, G1Y, G1P, G2X, G2Y, FX, FY, FD = range(13)
KINDS = 13


def step_kernel(
    x_hbm, h1_hbm, dy_hbm, wg_hbm, wu_hbm, wd_hbm, mg_hbm, mu_hbm, md_hbm, vg_hbm, vu_hbm, vd_hbm,
    wout, gout,
    h, a, at, ct, acc, wgv, wuv, wdv, actt, dgate, dup,
    grad, recv0, recv1, recv2, mbuf, vbuf, wbuf, wnew, gbuf,
    send_sem, recv_sem, load_sem, weight_sem, moment_sem, out_sem,
):
    rep, me = lax.axis_index("rep"), lax.axis_index("dp")
    c, qm = me % 2, me // 2
    qx, qy = (qm + 2) % 4, qm + 1 - 2 * (qm % 2)
    qd = (qy + 2) % 4
    partner, xn, yn = 2 * qm + 1 - c, 2 * qx + c, 2 * qy + c

    def remote(src, dst, kind, slot, device):
        return pltpu.make_async_remote_copy(
            src_ref=src, dst_ref=dst, send_sem=send_sem.at[kind, slot], recv_sem=recv_sem.at[kind, slot],
            device_id=(rep, device), device_id_type=pl.DeviceIdType.MESH,
        )

    half_p, half_q = pl.ds(0, R // 2), pl.ds(R // 2, R // 2)

    def copy_of(kind, u, slot):
        if kind == S0:
            return remote(grad.at[slot, 1 - c], recv0.at[slot], kind, slot, partner)
        if kind == S1X:
            return remote(grad.at[slot, c, qd, half_p], recv1.at[slot, 0], kind, slot, xn)
        if kind == S1Y:
            return remote(grad.at[slot, c, qd, half_q], recv1.at[slot, 1], kind, slot, yn)
        if kind == S2X:
            return remote(grad.at[slot, c, qx], recv2.at[slot, 0], kind, slot, xn)
        if kind == S2Y:
            return remote(grad.at[slot, c, qy], recv2.at[slot, 1], kind, slot, yn)
        if kind in (G1X, G1Y, G1P):
            to = {G1X: xn, G1Y: yn, G1P: partner}[kind]
            return remote(wnew.at[slot], wout.at[u, c, qm], kind, slot, to)
        if kind == G2X:
            return remote(wout.at[u, c, qy, half_p], wout.at[u, c, qy, half_p], kind, slot, xn)
        if kind == G2Y:
            return remote(wout.at[u, c, qx, half_q], wout.at[u, c, qx, half_q], kind, slot, yn)
        q = {FX: qx, FY: qy, FD: qd}[kind]
        return remote(wout.at[u, c, q], wout.at[u, c, q], kind, slot, partner)

    def own_copies(u, slot):
        return (
            pltpu.make_async_copy(wnew.at[slot], wout.at[u, c, qm], out_sem.at[0, slot]),
            pltpu.make_async_copy(gbuf.at[slot], gout.at[u], out_sem.at[1, slot]),
        )

    def rows(i):
        return pl.ds(pl.multiple_of(i * B, B), B)

    def start_weights(jj, half):
        layer, j = 1 - jj // 3, jj % 3
        for i in range(4):
            ff = pl.ds(pl.multiple_of((4 * half + i) * 384 + j * 128, 128), 128)
            here = pl.ds(i * 128, 128)
            pltpu.make_async_copy(wg_hbm.at[layer, :, ff], wgv.at[half, :, here], weight_sem.at[half, 0]).start()
            pltpu.make_async_copy(wu_hbm.at[layer, :, ff], wuv.at[half, :, here], weight_sem.at[half, 1]).start()
            pltpu.make_async_copy(wd_hbm.at[layer, ff, :], wdv.at[half, here, :], weight_sem.at[half, 2]).start()

    def wait_weights(half):
        pltpu.make_async_copy(wgv.at[half], wgv.at[half], weight_sem.at[half, 0]).wait()
        pltpu.make_async_copy(wuv.at[half], wuv.at[half], weight_sem.at[half, 1]).wait()
        pltpu.make_async_copy(wdv.at[half], wdv.at[half], weight_sem.at[half, 2]).wait()

    def start_moments(jj, k):
        layer, j = 1 - jj // 3, jj % 3
        mine = pl.ds(pl.multiple_of(me * 96, 32), 96)
        for n, (bufs, refs) in enumerate(
            ((mbuf, (mg_hbm, mu_hbm, md_hbm)), (vbuf, (vg_hbm, vu_hbm, vd_hbm)), (wbuf, (wg_hbm, wu_hbm, wd_hbm)))
        ):
            sem = moment_sem.at[k, n]
            if k < 2:
                for mat in range(2):
                    for i in range(4):
                        ff = pl.ds(pl.multiple_of((4 * k + i) * 384 + j * 128, 128), 128)
                        src = refs[mat].at[layer, mine if n == 2 else slice(None), ff]
                        pltpu.make_async_copy(src, bufs.at[k, pl.ds(96 * mat, 96), pl.ds(128 * i, 128)], sem).start()
            else:
                first = j * 128 if n < 2 else me * 384 + j * 128
                for row, count, col, width, to_row, to_col in (
                    (0, 128, 0, 512, 0, 0),
                    (0, 64, 512, 256, 128, 0),
                    (64, 64, 512, 256, 128, 256),
                ):
                    src = refs[2].at[layer, pl.ds(pl.multiple_of(first + row, 64), count), pl.ds(col, width)]
                    pltpu.make_async_copy(src, bufs.at[k, pl.ds(to_row, count), pl.ds(to_col, width)], sem).start()

    def wait_moments(k):
        for n, bufs in enumerate((mbuf, vbuf, wbuf)):
            pltpu.make_async_copy(bufs.at[k], bufs.at[k], moment_sem.at[k, n]).wait()

    def f32(ref_value):
        return ref_value.astype(F32)

    def gather_stage(stage, jj, k):
        u, slot = 3 * jj + k, 3 * (jj % 2) + k
        top, low = slice(0, R // 2), slice(R // 2, R)
        if stage == 1:
            copy_of(S0, u, slot).wait_recv()
            grad[slot, c, qd] = (f32(grad[slot, c, qd]) + f32(recv0[slot, qd])).astype(BF)
        if stage == 2:
            start_moments(jj, k)
            copy_of(S1X, u, slot).wait_recv()
            copy_of(S1Y, u, slot).wait_recv()
            for q, with_p in ((qy, True), (qx, False)):
                for part, is_p in ((top, True), (low, False)):
                    total = f32(grad[slot, c, q, part]) + f32(recv0[slot, q, part])
                    if is_p and with_p:
                        total += f32(recv1[slot, 0])
                    if not is_p and not with_p:
                        total += f32(recv1[slot, 1])
                    grad[slot, c, q, part] = total.astype(BF)
        if stage == 3:
            wait_moments(k)
            copy_of(S2X, u, slot).wait_recv()
            copy_of(S2Y, u, slot).wait_recv()
            for part in (top, low):
                g = f32(grad[slot, c, qm, part]) + f32(recv0[slot, qm, part])
                g = (g + f32(recv2[slot, 0, part]) + f32(recv2[slot, 1, part])).astype(BF)
                gbuf[slot, part] = g
                g = g.astype(F32)
                m = 0.9 * mbuf[k, part] + 0.1 * g
                v = 0.95 * vbuf[k, part] + 0.05 * g * g
                w = f32(wbuf[k, part])
                wnew[slot, part] = (w - 0.02 * (m * lax.rsqrt(v + 1e-8) + 0.1 * w)).astype(BF)
            for kind in (S0, S1X, S1Y, S2X, S2Y):
                copy_of(kind, u, slot).wait_send()

    def send_stage(stage, jj, k):
        u, slot = 3 * jj + k, 3 * (jj % 2) + k
        if stage == 1:
            copy_of(S1X, u, slot).start()
            copy_of(S1Y, u, slot).start()
        if stage == 2:
            copy_of(S2X, u, slot).start()
            copy_of(S2Y, u, slot).start()
        if stage == 3:
            for kind in (G1X, G1Y, G1P):
                copy_of(kind, u, slot).start()
            for copy in own_copies(u, slot):
                copy.start()
        if stage == 4:
            copy_of(G1X, u, slot).wait_recv()
            copy_of(G1Y, u, slot).wait_recv()
            for kind in (G2X, G2Y, FX, FY):
                copy_of(kind, u, slot).start()
        if stage == 5:
            copy_of(G2X, u, slot).wait_recv()
            copy_of(G2Y, u, slot).wait_recv()
            copy_of(FD, u, slot).start()
        if stage == 6:
            for kind in (G1P, FX, FY, FD):
                copy_of(kind, u, slot).wait_recv()
            for kind in (G1X, G1Y, G1P, G2X, G2Y, FX, FY, FD):
                copy_of(kind, u, slot).wait_send()
            for copy in own_copies(u, slot):
                copy.wait()

    def tick(jj, p):
        active = []
        for stage in (3, 2, 1, 4, 5, 6):
            q, r = divmod(p - LAG * stage, 6)
            if r in (1, 4, 5):
                active.append((stage, jj + q, {1: 0, 4: 1, 5: 2}[r]))
        for stage, unit_jj, k in active:
            if stage <= 3:

                @pl.when((unit_jj >= 0) & (unit_jj < 6))
                def _():
                    gather_stage(stage, unit_jj, k)

        if p in (1, 4, 5):

            @pl.when(jj < 6)
            def _():
                k = {1: 0, 4: 1, 5: 2}[p]
                copy_of(S0, 3 * jj + k, 3 * (jj % 2) + k).start()

        for stage, unit_jj, k in active:

            @pl.when((unit_jj >= 0) & (unit_jj < 6))
            def _():
                send_stage(stage, unit_jj, k)

    def norm_states():
        @pl.loop(0, T // B)
        def _(i):
            wide = h[rows(i), :].astype(F32)
            value = (wide * scale_of(wide)).astype(BF)
            a[rows(i), :] = value
            at[:, rows(i)] = value.T

    def piece_hidden(half):
        wait_weights(half)

        @pl.loop(0, T // B)
        def _(i):
            here = a[rows(i), :]
            gate = nn(here, wgv[half])
            up = nn(here, wuv[half])
            dact = nt(ct[rows(i), :], wdv[half]).astype(BF).astype(F32)
            sig = jax.nn.sigmoid(gate)
            silu = gate * sig
            actt[:, rows(i)] = (silu * up).astype(BF).T
            dup[rows(i), :] = (dact * silu).astype(BF)
            dgate[rows(i), :] = (dact * up * (sig * (1.0 + gate * (1.0 - sig)))).astype(BF)

    def piece_gate_up(jj, half):
        slot = 3 * (jj % 2) + half
        for mat, z in enumerate((dgate, dup)):
            for n in range(2):
                term = nn(at[pl.ds(n * 384, 384), :], z[...]).astype(BF)
                for i in range(4):
                    d = 4 * n + i
                    grad[slot, d % 2, d // 2, pl.ds(96 * mat, 96), :] = term[96 * i : 96 * (i + 1)]

    def piece_down(jj, half):
        slot = 3 * (jj % 2) + 2
        for n in range(2):
            term = nn(actt[pl.ds(n * 256, 256), :], ct[...]).astype(BF)
            for i in range(2):
                d = 4 * half + 2 * n + i
                block = term[128 * i : 128 * (i + 1)]
                grad[slot, d % 2, d // 2, pl.ds(0, 128), :] = block[:, :512]
                grad[slot, d % 2, d // 2, pl.ds(128, 64), pl.ds(0, 256)] = block[:64, 512:]
                grad[slot, d % 2, d // 2, pl.ds(128, 64), pl.ds(256, 256)] = block[64:, 512:]

        @pl.when(jj < 3)
        def _():
            @pl.loop(0, T // B)
            def _(i):
                acc[rows(i), :] += nt(dgate[rows(i), :], wgv[half]) + nt(dup[rows(i), :], wuv[half])

    def next_layer():
        @pl.loop(0, T // B)
        def _(i):
            wide = h[rows(i), :].astype(F32)
            scale = scale_of(wide)
            da = acc[rows(i), :].astype(BF).astype(F32)
            dot = jnp.mean(da * wide, -1, keepdims=True)
            dh = (da * scale - wide * (scale * scale * scale * dot)).astype(BF)
            ct[rows(i), :] = ct[rows(i), :] + dh

        load = pltpu.make_async_copy(x_hbm, h, load_sem.at[0])
        load.start()
        load.wait()
        norm_states()

    loads = [pltpu.make_async_copy(h1_hbm, h, load_sem.at[0]), pltpu.make_async_copy(dy_hbm, ct, load_sem.at[1])]
    for load in loads:
        load.start()
    start_weights(0, 0)
    barrier = pltpu.get_barrier_semaphore()
    for device in (partner, xn, yn):
        pl.semaphore_signal(barrier, inc=1, device_id=(rep, device), device_id_type=pl.DeviceIdType.MESH)
    for load in loads:
        load.wait()
    norm_states()
    acc[...] = jnp.zeros_like(acc)
    pl.semaphore_wait(barrier, 3)

    @pl.loop(0, 8)
    def _(jj):
        @pl.when(jj == 3)
        def _():
            next_layer()

        for half in range(2):

            @pl.when(jj < 6)
            def _():
                if half == 0:
                    start_weights(jj, 1)
                else:

                    @pl.when(jj < 5)
                    def _():
                        start_weights(jj + 1, 0)

                piece_hidden(half)

            tick(jj, 3 * half)

            @pl.when(jj < 6)
            def _():
                piece_gate_up(jj, half)

            tick(jj, 3 * half + 1)

            @pl.when(jj < 6)
            def _():
                piece_down(jj, half)

            tick(jj, 3 * half + 2)


def train_step(x, h1, dy, *arrays):
    anywhere = pl.BlockSpec(memory_space=pl.ANY)
    block = (R, S)
    return pl.pallas_call(
        step_kernel,
        out_shape=(
            jax.ShapeDtypeStruct((UNITS, 2, 4) + block, BF),
            jax.ShapeDtypeStruct((UNITS,) + block, BF),
        ),
        in_specs=[anywhere] * 12,
        out_specs=(anywhere, anywhere),
        scratch_shapes=[
            pltpu.VMEM((T, D), BF),
            pltpu.VMEM((T, D), BF),
            pltpu.VMEM((D, T), BF),
            pltpu.VMEM((T, D), BF),
            pltpu.VMEM((T, D), F32),
            pltpu.VMEM((2, D, S), BF),
            pltpu.VMEM((2, D, S), BF),
            pltpu.VMEM((2, S, D), BF),
            pltpu.VMEM((S, T), BF),
            pltpu.VMEM((T, S), BF),
            pltpu.VMEM((T, S), BF),
            pltpu.VMEM((NS, 2, 4) + block, BF),
            pltpu.VMEM((NS, 4) + block, BF),
            pltpu.VMEM((NS, 2, R // 2, S), BF),
            pltpu.VMEM((NS, 2) + block, BF),
            pltpu.VMEM((3,) + block, F32),
            pltpu.VMEM((3,) + block, F32),
            pltpu.VMEM((3,) + block, BF),
            pltpu.VMEM((NS,) + block, BF),
            pltpu.VMEM((NS,) + block, BF),
            pltpu.SemaphoreType.DMA((KINDS, NS)),
            pltpu.SemaphoreType.DMA((KINDS, NS)),
            pltpu.SemaphoreType.DMA((2,)),
            pltpu.SemaphoreType.DMA((2, 3)),
            pltpu.SemaphoreType.DMA((3, 3)),
            pltpu.SemaphoreType.DMA((2, NS)),
        ],
        compiler_params=pltpu.CompilerParams(
            collective_id=0, has_side_effects=True, vmem_limit_bytes=VMEM_LIMIT
        ),
        name="train_step",
    )(x, h1, dy, *arrays)


def columns_of(units):
    units = units[::-1]
    units = units.reshape(units.shape[:-1] + (4, 128))
    units = jnp.moveaxis(units, (1, 2), (-2, -4))
    return units.reshape(units.shape[:-4] + (FF,))


def rows_of(units):
    units = jnp.moveaxis(units[::-1], 1, -3)
    tail = jnp.concatenate((units[..., 128:, :256], units[..., 128:, 256:]), -2)
    return jnp.concatenate((units[..., :128, :], tail), -1)


def moments(m, v, g):
    g = g.astype(F32)
    return 0.9 * m + 0.1 * g, 0.95 * v + 0.05 * g * g


def solution(mesh):
    def body(x, dy, wg, wu, wd, mg, mu, md, vg, vu, vd):
        h1 = forward(x[0], wg, wu, wd)
        wout, gout = train_step(x[0], h1, dy[0], wg, wu, wd, mg, mu, md, vg, vu, vd)
        wout = wout.reshape(2, 3, 3, 2, 4, R, S).swapaxes(3, 4)
        gout = gout.reshape(2, 3, 3, R, S)
        new = [columns_of(wout[:, :, :2, :, :, i * 96 : i * 96 + 96, :]).reshape(2, D, FF) for i in range(2)]
        new.append(rows_of(wout[:, :, 2]).reshape(2, FF, D))
        g = [columns_of(gout[:, :, :2, i * 96 : i * 96 + 96, :]) for i in range(2)]
        g.append(rows_of(gout[:, :, 2]).reshape(2, 384, D))
        pairs = [moments(m, v, t) for m, v, t in zip((mg, mu, md), (vg, vu, vd), g)]
        return (*new, *(p[0] for p in pairs), *(p[1] for p in pairs))

    tok, whole, rows = P(("rep", "dp")), P(), P(None, "dp")
    return jax.shard_map(
        body,
        mesh=mesh,
        in_specs=(tok, tok) + (whole,) * 3 + (rows,) * 6,
        out_specs=(P("rep"),) * 3 + (P("rep", "dp"),) * 6,
        check_vma=False,
    )
```

time: 696 us -> 576 us (0.83)
  Pallas kernels: 0 us -> 323 us
  matrix products: 299 us -> 0 us
  waiting for transfers between devices: 284 us -> 0 us
  local copies, waits for them, and re-layouts: 35.7 us -> 227 us
  other arithmetic: 55.6 us -> 23.3 us
  between operations: 14.6 us -> 0.72 us
    pallas_call x0 -> x2, Pallas kernels: none -> 323 us  [the longest x1 280 us: train_step(): pl.pallas_call(step_kernel, out_shape=(jax.ShapeDtypeStruct((UNITS, 2, 4)...]
    dot_general x15 -> x0, matrix products: 299 us -> none  [the longest x5 115 us: layer(): gate = jnp.dot(a, wg, preferred_element_type=jnp.float32)]
    all_gather x6 -> x0, waiting for transfers between devices: 174 us -> none  [body(): new[i].append(lax.all_gather(nw, 'dp', axis=0, tiled=True))]
    reduce_scatter x6 -> x0, waiting for transfers between devices: 108 us -> none  [body(): lax.psum_scatter(grads[l][i], 'dp', scatter_dimension=0, tiled=True)]
    transpose x0 -> x3, local copies, waits for them, and re-layouts: none -> 59 us  [the longest x2 50.6 us: columns_of(): units = jnp.moveaxis(units, (1, 2), (-2, -4))]
    reshape x0 -> x3, local copies, waits for them, and re-layouts: none -> 47.2 us  [the longest x2 27.8 us: columns_of(): units = units.reshape(units.shape[:-1] + (4, 128))]
    another operation x0 -> x2, local copies, waits for them, and re-layouts: none -> 47.1 us  [body(): columns_of(wout[:, :, :2, :, :, i * 96:i * 96 + 96, :]).reshape(2, D, FF)]
    another operation x6 -> x0, other arithmetic: 34.7 us -> none  [body(): jnp.stack(t[i][::-1])]
  transfers between devices with their start and end apart: 12 -> 0, of which waited for: 9 -> 0; matrix products, arithmetic and copies ran while one was open for 32% -> 0% of each run, Pallas kernels for 0% -> 0%
where the time goes in v2:
time: 576 us; the launch traced here: 573 us
  Pallas kernels  323 us (56%)
  local copies, waits for them, and re-layouts  227 us (39%)
  other arithmetic  23.3 us (4%)
    pallas_call x1, Pallas kernels, train_step(): pl.pallas_call(step_kernel, out_shape=(jax.ShapeDtypeStruct((UNITS, 2, 4)...  280 us
    transpose x2, local copies, waits for them, and re-layouts, columns_of(): units = jnp.moveaxis(units, (1, 2), (-2, -4))  50.6 us
    another operation x2, local copies, waits for them, and re-layouts, body(): columns_of(wout[:, :, :2, :, :, i * 96:i * 96 + 96, :]).reshape(2, D, FF)  47.1 us
    pallas_call x1, Pallas kernels, forward(): pl.pallas_call(forward_kernel, grid=(FF // S,), out_shape=jax.ShapeDtypeS...  42.9 us
    reshape x2, local copies, waits for them, and re-layouts, columns_of(): units = units.reshape(units.shape[:-1] + (4, 128))  27.8 us
    reshape x1, local copies, waits for them, and re-layouts, body(): wout = wout.reshape(2, 3, 3, 2, 4, R, S).swapaxes(3, 4)  19.4 us
    rev x2, local copies, waits for them, and re-layouts, columns_of(): units = units[::-1]  17.2 us
    add x3, other arithmetic, moments(): return (0.9 * m + 0.1 * g, 0.95 * v + 0.05 * g * g)  16.1 us

profile of v2, /device:TPU:0, one launch (start us, length us, event | category | flops | bytes accessed | tf_op | source)
XLA Modules:
  0.0 573.2 jit_solution(3941401962644861119)
XLA Ops:
  0.6 42.9 %forward0.1.h1_hbm = bf16[2048,768]{1,0:T(8,128)(2,1)} custom-call(bf16[2048,768]{1,0:T(8,128)(2,1)} %bitcast.35, bf16[2,768,3072]{2,1,0:T(8,128)(2,1)} %wg_hbm.1, bf16[2,768,3072]{2,1,0:T(8,128)(2,1)} %wu_hbm.1, bf16[2,3072,768]{2,1,0:T(8,128)(2,1)} %wd_hbm.1), custom_call_target="tpu_custom_call" | custom-call | tf_op jit(solution)/shard_map/forward0/pallas_call | solution.py:63
  43.6 279.6 %train_step.1 = (bf16[18,2,4,192,512]{4,3,2,1,0:T(8,128)(2,1)}, bf16[18,192,512]{2,1,0:T(8,128)(2,1)}) custom-call(bf16[2048,768]{1,0:T(8,128)(2,1)} %bitcast.36, bf16[2048,768]{1,0:T(8,128)(2,1)} %forward0.1.h1_hbm, bf16[2048,768]{1,0:T(8,128)(2,1)} %bitcast.42, bf16[2,768,3072]{2,1,0:T(8,128)(2,1)} %wg_hbm.1, bf16[2,768,3072]{2,1,0:T(8,128)(2,1)} %wu_hbm.1, ...), custom_call_target="tpu_custom_call" | custom-call | tf_op jit(solution)/shard_map/train_step/pallas_call | solution.py:379
  323.2 19.4 %copy.33 = bf16[2,3,3,2,4,192,512]{6,5,3,4,2,1,0:T(8,128)(2,1)} copy(bf16[2,3,3,2,4,192,512]{6,5,4,3,2,1,0:T(8,128)(2,1)} %bitcast.34) | data formatting | bytes 56623104 | tf_op jit(solution)/shard_map/reshape | solution.py:444
  342.6 12.9 %fusion.4 = (bf16[2,3,2,4,2,96,512]{6,5,4,3,2,1,0:T(8,128)(2,1)}, bf16[2,3,2,4,2,96,512]{6,5,4,3,2,1,0:T(8,128)(2,1)}) fusion(bf16[2,3,3,4,2,192,512]{6,5,4,3,2,1,0:T(8,128)(2,1)} %bitcast.30), kind=kLoop, calls=%fused_computation.19 | loop fusion | bytes 37748736 | tf_op jit(solution)/shard_map/slice | solution.py:446
  355.5 8.6 %rev.16 = bf16[2,3,2,4,2,96,512]{6,5,4,3,2,1,0:T(8,128)(2,1)} reverse(bf16[2,3,2,4,2,96,512]{6,5,4,3,2,1,0:T(8,128)(2,1)} %get-tuple-element.14), dimensions={0} | reverse | bytes 18874368 | tf_op jit(solution)/shard_map/rev | solution.py:423
  364.2 13.9 %reshape.49 = bf16[2,3,2,4,2,96,4,128]{7,6,5,4,3,2,1,0:T(4,128)(2,1)} reshape(bf16[2,3,2,4,2,96,512]{6,5,4,3,2,1,0:T(8,128)(2,1)} %rev.16) | data formatting | bytes 18874368 | tf_op jit(solution)/shard_map/reshape | solution.py:424
  378.0 25.3 %copy.27 = bf16[2,4,2,96,2,4,3,128]{7,6,5,4,3,2,1,0:T(4,128)(2,1)} copy(bf16[2,4,2,96,2,4,3,128]{7,5,3,2,1,4,6,0:T(4,128)(2,1)} %bitcast.32) | data formatting | bytes 18874368 | tf_op jit(solution)/shard_map/transpose | solution.py:425
  403.3 23.5 %reshape_reshape.6 = bf16[2,768,3072]{2,1,0:T(8,128)(2,1)} reshape(bf16[2,4,2,96,2,4,3,128]{7,6,5,4,3,2,1,0:T(4,128)(2,1)} %copy.27) | data formatting | bytes 18874368 | tf_op jit(solution)/shard_map/reshape;reshape | solution.py:446
  426.9 8.6 %rev.17 = bf16[2,3,2,4,2,96,512]{6,5,4,3,2,1,0:T(8,128)(2,1)} reverse(bf16[2,3,2,4,2,96,512]{6,5,4,3,2,1,0:T(8,128)(2,1)} %get-tuple-element.13), dimensions={0} | reverse | bytes 18874368 | tf_op jit(solution)/shard_map/rev | solution.py:423
  435.5 13.9 %reshape.50 = bf16[2,3,2,4,2,96,4,128]{7,6,5,4,3,2,1,0:T(4,128)(2,1)} reshape(bf16[2,3,2,4,2,96,512]{6,5,4,3,2,1,0:T(8,128)(2,1)} %rev.17) | data formatting | bytes 18874368 | tf_op jit(solution)/shard_map/reshape | solution.py:424
  449.4 25.3 %copy.28 = bf16[2,4,2,96,2,4,3,128]{7,6,5,4,3,2,1,0:T(4,128)(2,1)} copy(bf16[2,4,2,96,2,4,3,128]{7,5,3,2,1,4,6,0:T(4,128)(2,1)} %bitcast.33) | data formatting | bytes 18874368 | tf_op jit(solution)/shard_map/transpose | solution.py:425
  474.7 23.5 %reshape_reshape.7 = bf16[2,768,3072]{2,1,0:T(8,128)(2,1)} reshape(bf16[2,4,2,96,2,4,3,128]{7,6,5,4,3,2,1,0:T(4,128)(2,1)} %copy.28) | data formatting | bytes 18874368 | tf_op jit(solution)/shard_map/reshape;reshape | solution.py:446
  498.2 8.5 %slice_bitcast_fusion = bf16[2,3,4,2,192,512]{5,4,3,2,1,0:T(8,128)(2,1)} fusion(bf16[2,3,3,4,2,192,512]{6,5,4,3,2,1,0:T(8,128)(2,1)} %bitcast.31), kind=kLoop, calls=%fused_computation.1 | loop fusion | bytes 18874368 | tf_op jit(solution)/shard_map/squeeze | solution.py:447
  506.7 8.4 %reverse_bitcast_fusion = bf16[2,4,2,3,192,512]{5,4,2,1,3,0:T(8,128)(2,1)} fusion(bf16[2,3,4,2,192,512]{5,4,3,2,1,0:T(8,128)(2,1)} %slice_bitcast_fusion), kind=kLoop, calls=%fused_computation.3 | loop fusion | bytes 18874368 | tf_op jit(solution)/shard_map/transpose | solution.py:430
  517.3 2.8 slice-done
  520.1 3.9 maximum_maximum_fusion
  524.0 8.6 %copy.29 = bf16[2,4,2,3,128,768]{5,4,3,2,1,0:T(8,128)(2,1)} copy(bf16[2,4,2,3,128,768]{5,4,2,1,3,0:T(8,128)(2,1)} %maximum_maximum_fusion) | data formatting | bytes 18874368 | tf_op jit(solution)/shard_map/concatenate | solution.py:432
  536.7 3.3 copy.30
  539.9 2.6 reshape.53
  542.5 6.6 %fusion = (f32[2,96,3072]{2,1,0:T(8,128)}, f32[2,96,3072]{2,1,0:T(8,128)}) fusion(f32[2,96,3072]{2,1,0:T(8,128)} %reshape.53, f32[2,96,3072]{2,1,0:T(8,128)} %vg_hbm.1, f32[2,96,3072]{2,1,0:T(8,128)} %mg_hbm.1), kind=kLoop, calls=%fused_computation.9 | loop fusion | flops 4128768 | bytes 11796480 | tf_op jit(solution)/shard_map/add | solution.py:437
  551.0 3.3 copy.31
  554.3 2.6 reshape.54
  556.9 6.5 %fusion.1 = (f32[2,96,3072]{2,1,0:T(8,128)}, f32[2,96,3072]{2,1,0:T(8,128)}) fusion(f32[2,96,3072]{2,1,0:T(8,128)} %reshape.54, f32[2,96,3072]{2,1,0:T(8,128)} %vu_hbm.1, f32[2,96,3072]{2,1,0:T(8,128)} %mu_hbm.1), kind=kLoop, calls=%fused_computation.10 | loop fusion | flops 4128768 | bytes 11796480 | tf_op jit(solution)/shard_map/add | solution.py:437
  570.3 3.0 fusion.3
  (21 shorter events, 14.8 us)
Async XLA Ops:
  517.2 2.8 slice-start
  524.0 8.6 %copy-start.3 = (bf16[18,192,512]{2,1,0:T(8,128)(2,1)S(1)}, bf16[18,192,512]{2,1,0:T(8,128)(2,1)}, u32[]{:S(2)}) copy-start(bf16[18,192,512]{2,1,0:T(8,128)(2,1)} %get-tuple-element.12) | copy-start | bytes 10616836
  542.5 6.7 %copy-start.2 = (f32[2,3,2,96,512]{4,3,2,1,0:T(8,128)S(1)}, f32[2,3,2,96,512]{4,3,2,1,0:T(8,128)}, u32[]{:S(2)}) copy-start(f32[2,3,2,96,512]{4,3,2,1,0:T(8,128)} %get-tuple-element.27) | copy-start | bytes 7077892
  566.2 3.5 copy-start
  568.4 1.9 copy-start.1

commit v3 on v2

--- a/solution.py
+++ b/solution.py
@@ -419,36 +419,62 @@
     )(x, h1, dy, *arrays)
 
 
-def columns_of(units):
-    units = units[::-1]
-    units = units.reshape(units.shape[:-1] + (4, 128))
-    units = jnp.moveaxis(units, (1, 2), (-2, -4))
-    return units.reshape(units.shape[:-4] + (FF,))
-
-
-def rows_of(units):
-    units = jnp.moveaxis(units[::-1], 1, -3)
-    tail = jnp.concatenate((units[..., 128:, :256], units[..., 128:, 256:]), -2)
-    return jnp.concatenate((units[..., :128, :], tail), -1)
-
-
-def moments(m, v, g):
-    g = g.astype(F32)
-    return 0.9 * m + 0.1 * g, 0.95 * v + 0.05 * g * g
+def unpack_kernel(w_ref, g_ref, mg, mu, md, vg, vu, vd, gate, up, down, new_mg, new_mu, new_md, new_vg, new_vu, new_vd):
+    d = pl.program_id(1)
+    for j in range(3):
+        for half in range(2):
+            for i in range(4):
+                to = pl.ds((4 * half + i) * 384 + j * 128, 128)
+                gate[0, :, to] = w_ref[0, 3 * j + half, 0, 0, :96, i * 128 : (i + 1) * 128]
+                up[0, :, to] = w_ref[0, 3 * j + half, 0, 0, 96:, i * 128 : (i + 1) * 128]
+        down[0, pl.ds(j * 128, 128), :512] = w_ref[0, 3 * j + 2, 0, 0, :128, :]
+        down[0, pl.ds(j * 128, 64), 512:] = w_ref[0, 3 * j + 2, 0, 0, 128:, :256]
+        down[0, pl.ds(j * 128 + 64, 64), 512:] = w_ref[0, 3 * j + 2, 0, 0, 128:, 256:]
+
+    def moments(g, m, v, new_m, new_v, at):
+        g = g.astype(F32)
+        new_m[at] = 0.9 * m[at] + 0.1 * g
+        new_v[at] = 0.95 * v[at] + 0.05 * g * g
+
+    lanes = pl.ds(pl.multiple_of((d % 4) * 128, 128), 128)
+    for j in range(3):
+        at = (0, slice(None), slice(j * 128, (j + 1) * 128))
+        moments(g_ref[0, 3 * j + d // 4, :96, lanes], mg, vg, new_mg, new_vg, at)
+        moments(g_ref[0, 3 * j + d // 4, 96:, lanes], mu, vu, new_mu, new_vu, at)
+
+    @pl.when(d < 3)
+    def _():
+        for row, count, col, width, to_row, to_col in ((0, 128, 0, 512, 0, 0), (128, 64, 0, 256, 0, 512), (128, 64, 256, 256, 64, 512)):
+            g = g_ref[0, 3 * d + 2, row : row + count, col : col + width]
+            moments(g, md, vd, new_md, new_vd, (0, slice(to_row, to_row + count), slice(to_col, to_col + width)))
+
+
+def unpack(wout, gout, mg, mu, md, vg, vu, vd):
+    w_spec = pl.BlockSpec((1, 9, 1, 1, R, S), lambda l, d: (1 - l, 0, d % 2, d // 2, 0, 0))
+    g_spec = pl.BlockSpec((1, 9, R, S), lambda l, d: (1 - l, 0, 0, 0))
+    wide = pl.BlockSpec((1, 96, FF), lambda l, d: (l, d, 0))
+    tall = pl.BlockSpec((1, 384, D), lambda l, d: (l, d, 0))
+    m_wide = pl.BlockSpec((1, 96, 384), lambda l, d: (l, 0, d))
+    m_tall = pl.BlockSpec((1, 128, D), lambda l, d: (l, jnp.minimum(d, 2), 0))
+    m_specs = [m_wide, m_wide, m_tall] * 2
+    moments = (mg, mu, md, vg, vu, vd)
+    return pl.pallas_call(
+        unpack_kernel,
+        grid=(2, 8),
+        out_shape=[jax.ShapeDtypeStruct(s, BF) for s in ((2, D, FF), (2, D, FF), (2, FF, D))]
+        + [jax.ShapeDtypeStruct(m.shape, F32) for m in moments],
+        in_specs=[w_spec, g_spec] + m_specs,
+        out_specs=[wide, wide, tall] + m_specs,
+        compiler_params=pltpu.CompilerParams(vmem_limit_bytes=56_000_000),
+        name="unpack",
+    )(wout.reshape(2, 9, 2, 4, R, S), gout.reshape(2, 9, R, S), *moments)
 
 
 def solution(mesh):
     def body(x, dy, wg, wu, wd, mg, mu, md, vg, vu, vd):
         h1 = forward(x[0], wg, wu, wd)
         wout, gout = train_step(x[0], h1, dy[0], wg, wu, wd, mg, mu, md, vg, vu, vd)
-        wout = wout.reshape(2, 3, 3, 2, 4, R, S).swapaxes(3, 4)
-        gout = gout.reshape(2, 3, 3, R, S)
-        new = [columns_of(wout[:, :, :2, :, :, i * 96 : i * 96 + 96, :]).reshape(2, D, FF) for i in range(2)]
-        new.append(rows_of(wout[:, :, 2]).reshape(2, FF, D))
-        g = [columns_of(gout[:, :, :2, i * 96 : i * 96 + 96, :]) for i in range(2)]
-        g.append(rows_of(gout[:, :, 2]).reshape(2, 384, D))
-        pairs = [moments(m, v, t) for m, v, t in zip((mg, mu, md), (vg, vu, vd), g)]
-        return (*new, *(p[0] for p in pairs), *(p[1] for p in pairs))
+        return tuple(unpack(wout, gout, mg, mu, md, vg, vu, vd))
 
     tok, whole, rows = P(("rep", "dp")), P(), P(None, "dp")
     return jax.shard_map(

time: 576 us -> 358 us (0.62)
  local copies, waits for them, and re-layouts: 227 us -> 0 us
  Pallas kernels: 323 us -> 357 us
  other arithmetic: 23.3 us -> 0 us
    transpose x3 -> x0, local copies, waits for them, and re-layouts: 59 us -> none  [the longest x2 50.6 us: columns_of(): units = jnp.moveaxis(units, (1, 2), (-2, -4))]
    reshape x3 -> x0, local copies, waits for them, and re-layouts: 47.2 us -> none  [the longest x2 27.8 us: columns_of(): units = units.reshape(units.shape[:-1] + (4, 128))]
    another operation x2 -> x0, local copies, waits for them, and re-layouts: 47.1 us -> none  [body(): columns_of(wout[:, :, :2, :, :, i * 96:i * 96 + 96, :]).reshape(2, D, FF)]
    pallas_call x0 -> x1, Pallas kernels: none -> 34.8 us  [unpack(): pl.pallas_call(unpack_kernel, grid=(2, 8), out_shape=[jax.ShapeDtypeStruc...]
    slice x10 -> x0, local copies, waits for them, and re-layouts: 21.7 us -> none  [the longest x1 12.9 us: body(): wout[:, :, :2, :, :, i * 96:i * 96 + 96, :]]
    rev x2 -> x0, local copies, waits for them, and re-layouts: 17.2 us -> none  [columns_of(): units = units[::-1]]
    add x3 -> x0, other arithmetic: 16.1 us -> none  [moments(): return (0.9 * m + 0.1 * g, 0.95 * v + 0.05 * g * g)]
    convert_element_type x6 -> x0, local copies, waits for them, and re-layouts: 15.4 us -> none  [moments(): g = g.astype(F32)]
where the time goes in v3:
time: 358 us
  Pallas kernels  357 us (100%)
    pallas_call x1, Pallas kernels, train_step(): pl.pallas_call(step_kernel, out_shape=(jax.ShapeDtypeStruct((UNITS, 2, 4)...  280 us
    pallas_call x1, Pallas kernels, forward(): pl.pallas_call(forward_kernel, grid=(FF // S,), out_shape=jax.ShapeDtypeS...  42.9 us
    pallas_call x1, Pallas kernels, unpack(): pl.pallas_call(unpack_kernel, grid=(2, 8), out_shape=[jax.ShapeDtypeStruc...  34.8 us

profile of v3, /device:TPU:0, one launch (start us, length us, event | category | flops | bytes accessed | tf_op | source)
XLA Modules:
  0.0 358.1 jit_solution(7260608272103092142)
XLA Ops:
  0.6 42.9 %forward0.1.h1_hbm = bf16[2048,768]{1,0:T(8,128)(2,1)} custom-call(bf16[2048,768]{1,0:T(8,128)(2,1)} %bitcast.5, bf16[2,768,3072]{2,1,0:T(8,128)(2,1)} %wg_hbm.1, bf16[2,768,3072]{2,1,0:T(8,128)(2,1)} %wu_hbm.1, bf16[2,3072,768]{2,1,0:T(8,128)(2,1)} %wd_hbm.1), custom_call_target="tpu_custom_call" | custom-call | tf_op jit(solution)/shard_map/forward0/pallas_call | solution.py:63
  43.6 279.6 %train_step.1 = (bf16[18,2,4,192,512]{4,3,2,1,0:T(8,128)(2,1)}, bf16[18,192,512]{2,1,0:T(8,128)(2,1)}) custom-call(bf16[2048,768]{1,0:T(8,128)(2,1)} %bitcast.6, bf16[2048,768]{1,0:T(8,128)(2,1)} %forward0.1.h1_hbm, bf16[2048,768]{1,0:T(8,128)(2,1)} %bitcast.8, bf16[2,768,3072]{2,1,0:T(8,128)(2,1)} %wg_hbm.1, bf16[2,768,3072]{2,1,0:T(8,128)(2,1)} %wu_hbm.1, ...), custom_call_target="tpu_custom_call" | custom-call | tf_op jit(solution)/shard_map/train_step/pallas_call | solution.py:379
  323.2 34.8 %unpack.1 = (bf16[2,768,3072]{2,1,0:T(8,128)(2,1)}, bf16[2,768,3072]{2,1,0:T(8,128)(2,1)}, bf16[2,3072,768]{2,1,0:T(8,128)(2,1)}, f32[2,96,3072]{2,1,0:T(8,128)}...) custom-call(bf16[2,9,2,4,192,512]{5,4,3,2,1,0:T(8,128)(2,1)} %bitcas, ...), custom_call_target="tpu_custom_call" | custom-call | tf_op jit(solution)/shard_map/unpack/pallas_call | solution.py:461

commit v4 on v3

--- a/solution.py
+++ b/solution.py
@@ -10,7 +10,7 @@
 B = 512
 R = 192
 NS = 6
-LAG = 2
+LAGS = (0, 1, 2, 4, 6, 8, 10)
 UNITS = 18
 VMEM_LIMIT = 66_500_000
 BF, F32 = jnp.bfloat16, jnp.float32
@@ -28,56 +28,12 @@
     return lax.rsqrt(jnp.mean(wide * wide, -1, keepdims=True) + 1e-6)
 
 
-def forward_kernel(x_ref, wg_ref, wu_ref, wd_ref, out_ref, a_ref, acc_ref):
-    t = pl.program_id(0)
-
-    def rows(i):
-        return pl.ds(pl.multiple_of(i * B, B), B)
-
-    @pl.when(t == 0)
-    def _():
-        @pl.loop(0, T // B)
-        def _(i):
-            wide = x_ref[rows(i), :].astype(F32)
-            a_ref[rows(i), :] = (wide * scale_of(wide)).astype(BF)
-            acc_ref[rows(i), :] = jnp.zeros((B, D), F32)
-
-    @pl.loop(0, T // B)
-    def _(i):
-        a = a_ref[rows(i), :]
-        gate = nn(a, wg_ref[0])
-        up = nn(a, wu_ref[0])
-        act = (gate * jax.nn.sigmoid(gate) * up).astype(BF)
-        acc_ref[rows(i), :] += nn(act, wd_ref[0])
-
-    @pl.when(t == pl.num_programs(0) - 1)
-    def _():
-        @pl.loop(0, T // B)
-        def _(i):
-            out_ref[rows(i), :] = x_ref[rows(i), :] + acc_ref[rows(i), :].astype(BF)
-
-
-def forward(x, wg, wu, wd):
-    whole = pl.BlockSpec((T, D), lambda t: (0, 0))
-    cols = pl.BlockSpec((1, D, S), lambda t: (0, 0, t))
-    return pl.pallas_call(
-        forward_kernel,
-        grid=(FF // S,),
-        out_shape=jax.ShapeDtypeStruct((T, D), BF),
-        in_specs=[whole, cols, cols, pl.BlockSpec((1, S, D), lambda t: (0, t, 0))],
-        out_specs=whole,
-        scratch_shapes=[pltpu.VMEM((T, D), BF), pltpu.VMEM((T, D), F32)],
-        compiler_params=pltpu.CompilerParams(vmem_limit_bytes=56_000_000),
-        name="forward0",
-    )(x, wg, wu, wd)
-
-
 S0, S1X, S1Y, S2X, S2Y, G1X, G1Y, G1P, G2X, G2Y, FX, FY, FD = range(13)
 KINDS = 13
 
 
 def step_kernel(
-    x_hbm, h1_hbm, dy_hbm, wg_hbm, wu_hbm, wd_hbm, mg_hbm, mu_hbm, md_hbm, vg_hbm, vu_hbm, vd_hbm,
+    x_hbm, dy_hbm, wg_hbm, wu_hbm, wd_hbm, mg_hbm, mu_hbm, md_hbm, vg_hbm, vu_hbm, vd_hbm,
     wout, gout,
     h, a, at, ct, acc, wgv, wuv, wdv, actt, dgate, dup,
     grad, recv0, recv1, recv2, mbuf, vbuf, wbuf, wnew, gbuf,
@@ -237,8 +193,8 @@
 
     def tick(jj, p):
         active = []
-        for stage in (3, 2, 1, 4, 5, 6):
-            q, r = divmod(p - LAG * stage, 6)
+        for stage in range(1, 7):
+            q, r = divmod(p - LAGS[stage], 6)
             if r in (1, 4, 5):
                 active.append((stage, jj + q, {1: 0, 4: 1, 5: 2}[r]))
         for stage, unit_jj, k in active:
@@ -325,17 +281,60 @@
         load.wait()
         norm_states()
 
-    loads = [pltpu.make_async_copy(h1_hbm, h, load_sem.at[0]), pltpu.make_async_copy(dy_hbm, ct, load_sem.at[1])]
-    for load in loads:
-        load.start()
-    start_weights(0, 0)
+    def start_forward(block, half):
+        ff = pl.ds(pl.multiple_of(block * S, S), S)
+        pltpu.make_async_copy(wg_hbm.at[0, :, ff], wgv.at[half], weight_sem.at[half, 0]).start()
+        pltpu.make_async_copy(wu_hbm.at[0, :, ff], wuv.at[half], weight_sem.at[half, 1]).start()
+        pltpu.make_async_copy(wd_hbm.at[0, ff, :], wdv.at[half], weight_sem.at[half, 2]).start()
+
+    def piece_forward(half):
+        wait_weights(half)
+
+        @pl.loop(0, T // B)
+        def _(i):
+            here = a[rows(i), :]
+            gate = nn(here, wgv[half])
+            up = nn(here, wuv[half])
+            act = (gate * jax.nn.sigmoid(gate) * up).astype(BF)
+            acc[rows(i), :] += nn(act, wdv[half])
+
+    loads = [pltpu.make_async_copy(x_hbm, h, load_sem.at[0]), pltpu.make_async_copy(dy_hbm, ct, load_sem.at[1])]
+    loads[0].start()
+    start_forward(0, 0)
+    loads[1].start()
     barrier = pltpu.get_barrier_semaphore()
     for device in (partner, xn, yn):
         pl.semaphore_signal(barrier, inc=1, device_id=(rep, device), device_id_type=pl.DeviceIdType.MESH)
-    for load in loads:
-        load.wait()
+    loads[0].wait()
+
+    @pl.loop(0, T // B)
+    def _(i):
+        wide = h[rows(i), :].astype(F32)
+        a[rows(i), :] = (wide * scale_of(wide)).astype(BF)
+        acc[rows(i), :] = jnp.zeros((B, D), F32)
+
+    @pl.loop(0, FF // S // 2)
+    def _(pair):
+        start_forward(2 * pair + 1, 1)
+        piece_forward(0)
+
+        @pl.when(pair < FF // S // 2 - 1)
+        def _():
+            start_forward(2 * pair + 2, 0)
+
+        @pl.when(pair == FF // S // 2 - 1)
+        def _():
+            start_weights(0, 0)
+
+        piece_forward(1)
+
+    @pl.loop(0, T // B)
+    def _(i):
+        h[rows(i), :] = h[rows(i), :] + acc[rows(i), :].astype(BF)
+        acc[rows(i), :] = jnp.zeros((B, D), F32)
+
     norm_states()
-    acc[...] = jnp.zeros_like(acc)
+    loads[1].wait()
     pl.semaphore_wait(barrier, 3)
 
     @pl.loop(0, 8)
@@ -373,7 +372,7 @@
             tick(jj, 3 * half + 2)
 
 
-def train_step(x, h1, dy, *arrays):
+def train_step(x, dy, *arrays):
     anywhere = pl.BlockSpec(memory_space=pl.ANY)
     block = (R, S)
     return pl.pallas_call(
@@ -382,7 +381,7 @@
             jax.ShapeDtypeStruct((UNITS, 2, 4) + block, BF),
             jax.ShapeDtypeStruct((UNITS,) + block, BF),
         ),
-        in_specs=[anywhere] * 12,
+        in_specs=[anywhere] * 11,
         out_specs=(anywhere, anywhere),
         scratch_shapes=[
             pltpu.VMEM((T, D), BF),
@@ -416,7 +415,7 @@
             collective_id=0, has_side_effects=True, vmem_limit_bytes=VMEM_LIMIT
         ),
         name="train_step",
-    )(x, h1, dy, *arrays)
+    )(x, dy, *arrays)
 
 
 def unpack_kernel(w_ref, g_ref, mg, mu, md, vg, vu, vd, gate, up, down, new_mg, new_mu, new_md, new_vg, new_vu, new_vd):
@@ -472,8 +471,7 @@
 
 def solution(mesh):
     def body(x, dy, wg, wu, wd, mg, mu, md, vg, vu, vd):
-        h1 = forward(x[0], wg, wu, wd)
-        wout, gout = train_step(x[0], h1, dy[0], wg, wu, wd, mg, mu, md, vg, vu, vd)
+        wout, gout = train_step(x[0], dy[0], wg, wu, wd, mg, mu, md, vg, vu, vd)
         return tuple(unpack(wout, gout, mg, mu, md, vg, vu, vd))
 
     tok, whole, rows = P(("rep", "dp")), P(), P(None, "dp")

time: 358 us -> 345 us (0.964)
  Pallas kernels: 357 us -> 344 us
    pallas_call x1 -> x0, Pallas kernels: 42.9 us -> none  [forward(): pl.pallas_call(forward_kernel, grid=(FF // S,), out_shape=jax.ShapeDtypeS...]
    pallas_call x1, Pallas kernels: 280 us -> 309 us  [train_step(): pl.pallas_call(step_kernel, out_shape=(jax.ShapeDtypeStruct((UNITS, 2, 4)...]
where the time goes in v4:
time: 345 us; the launch traced here: 344 us
  Pallas kernels  344 us (100%)
    pallas_call x1, Pallas kernels, train_step(): pl.pallas_call(step_kernel, out_shape=(jax.ShapeDtypeStruct((UNITS, 2, 4)...  309 us
    pallas_call x1, Pallas kernels, unpack(): pl.pallas_call(unpack_kernel, grid=(2, 8), out_shape=[jax.ShapeDtypeStruc...  34.8 us

profile of v4, /device:TPU:0, one launch (start us, length us, event | category | flops | bytes accessed | tf_op | source)
XLA Modules:
  0.0 344.4 jit_solution(17716685696714373336)
XLA Ops:
  0.6 308.9 %train_step.1 = (bf16[18,2,4,192,512]{4,3,2,1,0:T(8,128)(2,1)}, bf16[18,192,512]{2,1,0:T(8,128)(2,1)}) custom-call(bf16[2048,768]{1,0:T(8,128)(2,1)} %bitcast.6, bf16[2048,768]{1,0:T(8,128)(2,1)} %bitcast.7, bf16[2,768,3072]{2,1,0:T(8,128)(2,1)} %wg_hbm.1, bf16[2,768,3072]{2,1,0:T(8,128)(2,1)} %wu_hbm.1, bf16[2,3072,768]{2,1,0:T(8,128)(2,1)} %wd_hbm.1, ...), custom_call_target="tpu_custom_call" | custom-call | tf_op jit(solution)/shard_map/train_step/pallas_call | solution.py:378
  309.5 34.8 %unpack.1 = (bf16[2,768,3072]{2,1,0:T(8,128)(2,1)}, bf16[2,768,3072]{2,1,0:T(8,128)(2,1)}, bf16[2,3072,768]{2,1,0:T(8,128)(2,1)}, f32[2,96,3072]{2,1,0:T(8,128)}...) custom-call(bf16[2,9,2,4,192,512]{5,4,3,2,1,0:T(8,128)(2,1)} %bitcas, ...), custom_call_target="tpu_custom_call" | custom-call | tf_op jit(solution)/shard_map/unpack/pallas_call | solution.py:460

commit v5 on v4

--- a/solution.py
+++ b/solution.py
@@ -418,53 +418,137 @@
     )(x, dy, *arrays)
 
 
-def unpack_kernel(w_ref, g_ref, mg, mu, md, vg, vu, vd, gate, up, down, new_mg, new_mu, new_md, new_vg, new_vu, new_vd):
-    d = pl.program_id(1)
-    for j in range(3):
-        for half in range(2):
-            for i in range(4):
-                to = pl.ds((4 * half + i) * 384 + j * 128, 128)
-                gate[0, :, to] = w_ref[0, 3 * j + half, 0, 0, :96, i * 128 : (i + 1) * 128]
-                up[0, :, to] = w_ref[0, 3 * j + half, 0, 0, 96:, i * 128 : (i + 1) * 128]
-        down[0, pl.ds(j * 128, 128), :512] = w_ref[0, 3 * j + 2, 0, 0, :128, :]
-        down[0, pl.ds(j * 128, 64), 512:] = w_ref[0, 3 * j + 2, 0, 0, 128:, :256]
-        down[0, pl.ds(j * 128 + 64, 64), 512:] = w_ref[0, 3 * j + 2, 0, 0, 128:, 256:]
-
-    def moments(g, m, v, new_m, new_v, at):
+def unpack_kernel(
+    w_hbm, g_hbm, mg, mu, md, vg, vu, vd,
+    gate, up, down, new_mg, new_mu, new_md, new_vg, new_vu, new_vd,
+    held, g_ref, wide, tall, out_wide, out_tall, held_sem, g_sem, load_sem, out_sem, store_sem,
+):
+    wides, talls = (mg, mu, vg, vu), (md, vd)
+    new_wides, new_talls = (new_mg, new_mu, new_vg, new_vu), (new_md, new_vd)
+
+    def load_block(n):
+        return pltpu.make_async_copy(w_hbm.at[1 - n // 8, :, n % 2, (n % 8) // 2], held.at[n], held_sem.at[n])
+
+    def load_layer(layer):
+        copies = [pltpu.make_async_copy(g_hbm.at[1 - layer], g_ref.at[layer], g_sem.at[layer])]
+        for i, ref in enumerate(wides):
+            copies.append(pltpu.make_async_copy(ref.at[layer], wide.at[i, layer], load_sem.at[layer, i]))
+        for i, ref in enumerate(talls):
+            copies.append(pltpu.make_async_copy(ref.at[layer], tall.at[i, layer], load_sem.at[layer, 4 + i]))
+        return copies
+
+    def stores(n):
+        layer, d, slot = n // 8, n % 8, n % 4
+        few, many = pl.ds(pl.multiple_of(d * 96, 32), 96), pl.ds(pl.multiple_of(d * 384, 128), 384)
+        return (
+            pltpu.make_async_copy(out_wide.at[slot, 0], gate.at[layer, few], out_sem.at[slot, 0]),
+            pltpu.make_async_copy(out_wide.at[slot, 1], up.at[layer, few], out_sem.at[slot, 1]),
+            pltpu.make_async_copy(out_tall.at[slot], down.at[layer, many], out_sem.at[slot, 2]),
+        )
+
+    def moments(g, m_ref, v_ref, at):
         g = g.astype(F32)
-        new_m[at] = 0.9 * m[at] + 0.1 * g
-        new_v[at] = 0.95 * v[at] + 0.05 * g * g
-
-    lanes = pl.ds(pl.multiple_of((d % 4) * 128, 128), 128)
-    for j in range(3):
-        at = (0, slice(None), slice(j * 128, (j + 1) * 128))
-        moments(g_ref[0, 3 * j + d // 4, :96, lanes], mg, vg, new_mg, new_vg, at)
-        moments(g_ref[0, 3 * j + d // 4, 96:, lanes], mu, vu, new_mu, new_vu, at)
-
-    @pl.when(d < 3)
-    def _():
-        for row, count, col, width, to_row, to_col in ((0, 128, 0, 512, 0, 0), (128, 64, 0, 256, 0, 512), (128, 64, 256, 256, 64, 512)):
-            g = g_ref[0, 3 * d + 2, row : row + count, col : col + width]
-            moments(g, md, vd, new_md, new_vd, (0, slice(to_row, to_row + count), slice(to_col, to_col + width)))
-
-
-def unpack(wout, gout, mg, mu, md, vg, vu, vd):
-    w_spec = pl.BlockSpec((1, 9, 1, 1, R, S), lambda l, d: (1 - l, 0, d % 2, d // 2, 0, 0))
-    g_spec = pl.BlockSpec((1, 9, R, S), lambda l, d: (1 - l, 0, 0, 0))
-    wide = pl.BlockSpec((1, 96, FF), lambda l, d: (l, d, 0))
-    tall = pl.BlockSpec((1, 384, D), lambda l, d: (l, d, 0))
-    m_wide = pl.BlockSpec((1, 96, 384), lambda l, d: (l, 0, d))
-    m_tall = pl.BlockSpec((1, 128, D), lambda l, d: (l, jnp.minimum(d, 2), 0))
-    m_specs = [m_wide, m_wide, m_tall] * 2
-    moments = (mg, mu, md, vg, vu, vd)
+        m_ref[at] = 0.9 * m_ref[at] + 0.1 * g
+        v_ref[at] = 0.95 * v_ref[at] + 0.05 * g * g
+
+    load_block(0).start()
+    load_block(1).start()
+    for copy in load_layer(0):
+        copy.start()
+
+    @pl.loop(2, 8)
+    def _(n):
+        load_block(n).start()
+
+    for copy in load_layer(1):
+        copy.start()
+
+    @pl.loop(8, 16)
+    def _(n):
+        load_block(n).start()
+
+    @pl.loop(0, 16)
+    def _(n):
+        layer, d, slot = n // 8, n % 8, n % 4
+
+        @pl.when(n >= 4)
+        def _():
+            for copy in stores(n - 4):
+                copy.wait()
+
+        load_block(n).wait()
+        for j in range(3):
+            for half in range(2):
+                for i in range(4):
+                    to = pl.ds((4 * half + i) * 384 + j * 128, 128)
+                    out_wide[slot, 0, :, to] = held[n, 3 * j + half, :96, i * 128 : (i + 1) * 128]
+                    out_wide[slot, 1, :, to] = held[n, 3 * j + half, 96:, i * 128 : (i + 1) * 128]
+            out_tall[slot, pl.ds(j * 128, 128), :512] = held[n, 3 * j + 2, :128, :]
+            out_tall[slot, pl.ds(j * 128, 64), 512:] = held[n, 3 * j + 2, 128:, :256]
+            out_tall[slot, pl.ds(j * 128 + 64, 64), 512:] = held[n, 3 * j + 2, 128:, 256:]
+        for copy in stores(n):
+            copy.start()
+
+        for first in range(2):
+
+            @pl.when(n == 8 * first)
+            def _():
+                for copy in load_layer(first):
+                    copy.wait()
+
+        lanes = pl.ds(pl.multiple_of((d % 4) * 128, 128), 128)
+        block = pl.ds(pl.multiple_of(d * 384, 128), 384)
+        for mat in range(2):
+            for j in range(3):
+                at = (layer, slice(None), pl.ds(pl.multiple_of(d * 384 + j * 128, 128), 128))
+                g = g_ref[layer, 3 * j + d // 4, 96 * mat : 96 * (mat + 1), lanes]
+                moments(g, wide.at[mat], wide.at[2 + mat], at)
+        for i, ref in enumerate(new_wides):
+            pltpu.make_async_copy(wide.at[i, layer, :, block], ref.at[layer, :, block], store_sem.at[i]).start()
+
+        @pl.when(d < 3)
+        def _():
+            rows = pl.ds(pl.multiple_of(d * 128, 128), 128)
+            for row, count, col, width, to_row, to_col in ((0, 128, 0, 512, 0, 0), (128, 64, 0, 256, 0, 512), (128, 64, 256, 256, 64, 512)):
+                g = g_ref[layer, 3 * d + 2, row : row + count, col : col + width]
+                at = (layer, pl.ds(pl.multiple_of(d * 128 + to_row, 64), count), slice(to_col, to_col + width))
+                moments(g, tall.at[0], tall.at[1], at)
+            for i, ref in enumerate(new_talls):
+                pltpu.make_async_copy(tall.at[i, layer, rows], ref.at[layer, rows], store_sem.at[4 + i]).start()
+
+    @pl.loop(12, 16)
+    def _(n):
+        for copy in stores(n):
+            copy.wait()
+
+    for i, ref in enumerate(new_wides):
+        pltpu.make_async_copy(wide.at[i], ref, store_sem.at[i]).wait()
+    for i, ref in enumerate(new_talls):
+        pltpu.make_async_copy(tall.at[i], ref, store_sem.at[4 + i]).wait()
+
+
+def unpack(wout, gout, *moments):
+    anywhere = pl.BlockSpec(memory_space=pl.ANY)
     return pl.pallas_call(
         unpack_kernel,
-        grid=(2, 8),
         out_shape=[jax.ShapeDtypeStruct(s, BF) for s in ((2, D, FF), (2, D, FF), (2, FF, D))]
         + [jax.ShapeDtypeStruct(m.shape, F32) for m in moments],
-        in_specs=[w_spec, g_spec] + m_specs,
-        out_specs=[wide, wide, tall] + m_specs,
-        compiler_params=pltpu.CompilerParams(vmem_limit_bytes=56_000_000),
+        in_specs=[anywhere] * 8,
+        out_specs=[anywhere] * 9,
+        scratch_shapes=[
+            pltpu.VMEM((16, 9, R, S), BF),
+            pltpu.VMEM((2, 9, R, S), BF),
+            pltpu.VMEM((4, 2, 96, FF), F32),
+            pltpu.VMEM((2, 2, 384, D), F32),
+            pltpu.VMEM((4, 2, 96, FF), BF),
+            pltpu.VMEM((4, 384, D), BF),
+            pltpu.SemaphoreType.DMA((16,)),
+            pltpu.SemaphoreType.DMA((2,)),
+            pltpu.SemaphoreType.DMA((2, 6)),
+            pltpu.SemaphoreType.DMA((4, 3)),
+            pltpu.SemaphoreType.DMA((6,)),
+        ],
+        compiler_params=pltpu.CompilerParams(vmem_limit_bytes=VMEM_LIMIT),
         name="unpack",
     )(wout.reshape(2, 9, 2, 4, R, S), gout.reshape(2, 9, R, S), *moments)
 

time: 345 us -> 339 us (0.983)
  Pallas kernels: 344 us -> 338 us
    pallas_call x1, Pallas kernels: 34.8 us -> 28.7 us  [unpack(): pl.pallas_call(unpack_kernel, out_shape=[jax.ShapeDtypeStruct(s, BF) for...]
where the time goes in v5:
time: 339 us; the launch traced here: 338 us
  Pallas kernels  338 us (100%)
    pallas_call x1, Pallas kernels, train_step(): pl.pallas_call(step_kernel, out_shape=(jax.ShapeDtypeStruct((UNITS, 2, 4)...  309 us
    pallas_call x1, Pallas kernels, unpack(): pl.pallas_call(unpack_kernel, out_shape=[jax.ShapeDtypeStruct(s, BF) for...  28.7 us

profile of v5, /device:TPU:0, one launch (start us, length us, event | category | flops | bytes accessed | tf_op | source)
XLA Modules:
  0.0 338.4 jit_solution(17993494209301774058)
XLA Ops:
  0.6 308.9 %train_step.1 = (bf16[18,2,4,192,512]{4,3,2,1,0:T(8,128)(2,1)}, bf16[18,192,512]{2,1,0:T(8,128)(2,1)}) custom-call(bf16[2048,768]{1,0:T(8,128)(2,1)} %bitcast.6, bf16[2048,768]{1,0:T(8,128)(2,1)} %bitcast.7, bf16[2,768,3072]{2,1,0:T(8,128)(2,1)} %wg_hbm.1, bf16[2,768,3072]{2,1,0:T(8,128)(2,1)} %wu_hbm.1, bf16[2,3072,768]{2,1,0:T(8,128)(2,1)} %wd_hbm.1, ...), custom_call_target="tpu_custom_call" | custom-call | tf_op jit(solution)/shard_map/train_step/pallas_call | solution.py:378
  309.5 28.7 %unpack.1 = (bf16[2,768,3072]{2,1,0:T(8,128)(2,1)}, bf16[2,768,3072]{2,1,0:T(8,128)(2,1)}, bf16[2,3072,768]{2,1,0:T(8,128)(2,1)}, f32[2,96,3072]{2,1,0:T(8,128)}...) custom-call(bf16[2,9,2,4,192,512]{5,4,3,2,1,0:T(8,128)(2,1)} %bitcas, ...), custom_call_target="tpu_custom_call" | custom-call | tf_op jit(solution)/shard_map/unpack/pallas_call | solution.py:532

commit v6 on v5

--- a/solution.py
+++ b/solution.py
@@ -8,9 +8,10 @@
 T, D, FF = 2048, 768, 3072
 S = 512
 B = 512
+TICKS = 8
 R = 192
 NS = 6
-LAGS = (0, 1, 2, 4, 6, 8, 10)
+LAGS = (0, 1, 3, 5, 7, 10, 11)
 UNITS = 18
 VMEM_LIMIT = 66_500_000
 BF, F32 = jnp.bfloat16, jnp.float32
@@ -194,7 +195,7 @@
     def tick(jj, p):
         active = []
         for stage in range(1, 7):
-            q, r = divmod(p - LAGS[stage], 6)
+            q, r = divmod(p - LAGS[stage], TICKS)
             if r in (1, 4, 5):
                 active.append((stage, jj + q, {1: 0, 4: 1, 5: 2}[r]))
         for stage, unit_jj, k in active:
@@ -237,14 +238,14 @@
             sig = jax.nn.sigmoid(gate)
             silu = gate * sig
             actt[:, rows(i)] = (silu * up).astype(BF).T
-            dup[rows(i), :] = (dact * silu).astype(BF)
-            dgate[rows(i), :] = (dact * up * (sig * (1.0 + gate * (1.0 - sig)))).astype(BF)
+            dup[half, rows(i), :] = (dact * silu).astype(BF)
+            dgate[half, rows(i), :] = (dact * up * (sig * (1.0 + gate * (1.0 - sig)))).astype(BF)
 
     def piece_gate_up(jj, half):
         slot = 3 * (jj % 2) + half
         for mat, z in enumerate((dgate, dup)):
             for n in range(2):
-                term = nn(at[pl.ds(n * 384, 384), :], z[...]).astype(BF)
+                term = nn(at[pl.ds(n * 384, 384), :], z[half]).astype(BF)
                 for i in range(4):
                     d = 4 * n + i
                     grad[slot, d % 2, d // 2, pl.ds(96 * mat, 96), :] = term[96 * i : 96 * (i + 1)]
@@ -260,11 +261,10 @@
                 grad[slot, d % 2, d // 2, pl.ds(128, 64), pl.ds(0, 256)] = block[:64, 512:]
                 grad[slot, d % 2, d // 2, pl.ds(128, 64), pl.ds(256, 256)] = block[64:, 512:]
 
-        @pl.when(jj < 3)
-        def _():
-            @pl.loop(0, T // B)
-            def _(i):
-                acc[rows(i), :] += nt(dgate[rows(i), :], wgv[half]) + nt(dup[rows(i), :], wuv[half])
+    def piece_states(half):
+        @pl.loop(0, T // B)
+        def _(i):
+            acc[rows(i), :] += nt(dgate[half, rows(i), :], wgv[half]) + nt(dup[half, rows(i), :], wuv[half])
 
     def next_layer():
         @pl.loop(0, T // B)
@@ -275,10 +275,9 @@
             dot = jnp.mean(da * wide, -1, keepdims=True)
             dh = (da * scale - wide * (scale * scale * scale * dot)).astype(BF)
             ct[rows(i), :] = ct[rows(i), :] + dh
-
-        load = pltpu.make_async_copy(x_hbm, h, load_sem.at[0])
-        load.start()
-        load.wait()
+            pltpu.make_async_copy(x_hbm.at[rows(i)], h.at[rows(i)], load_sem.at[0]).start()
+
+        pltpu.make_async_copy(x_hbm, h, load_sem.at[0]).wait()
         norm_states()
 
     def start_forward(block, half):
@@ -349,12 +348,6 @@
             def _():
                 if half == 0:
                     start_weights(jj, 1)
-                else:
-
-                    @pl.when(jj < 5)
-                    def _():
-                        start_weights(jj + 1, 0)
-
                 piece_hidden(half)
 
             tick(jj, 3 * half)
@@ -370,6 +363,20 @@
                 piece_down(jj, half)
 
             tick(jj, 3 * half + 2)
+
+        for half in range(2):
+
+            @pl.when(jj < 3)
+            def _():
+                piece_states(half)
+
+            if half == 0:
+
+                @pl.when(jj < 5)
+                def _():
+                    start_weights(jj + 1, 0)
+
+            tick(jj, 6 + half)
 
 
 def train_step(x, dy, *arrays):
@@ -393,8 +400,8 @@
             pltpu.VMEM((2, D, S), BF),
             pltpu.VMEM((2, S, D), BF),
             pltpu.VMEM((S, T), BF),
-            pltpu.VMEM((T, S), BF),
-            pltpu.VMEM((T, S), BF),
+            pltpu.VMEM((2, T, S), BF),
+            pltpu.VMEM((2, T, S), BF),
             pltpu.VMEM((NS, 2, 4) + block, BF),
             pltpu.VMEM((NS, 4) + block, BF),
             pltpu.VMEM((NS, 2, R // 2, S), BF),

time: 339 us -> 332 us (0.979)
  Pallas kernels: 338 us -> 331 us
    pallas_call x1, Pallas kernels: 309 us -> 302 us  [train_step(): pl.pallas_call(step_kernel, out_shape=(jax.ShapeDtypeStruct((UNITS, 2, 4)...]
where the time goes in v6:
time: 332 us
  Pallas kernels  331 us (100%)
    pallas_call x1, Pallas kernels, train_step(): pl.pallas_call(step_kernel, out_shape=(jax.ShapeDtypeStruct((UNITS, 2, 4)...  302 us
    pallas_call x1, Pallas kernels, unpack(): pl.pallas_call(unpack_kernel, out_shape=[jax.ShapeDtypeStruct(s, BF) for...  28.7 us

profile of v6, /device:TPU:0, one launch (start us, length us, event | category | flops | bytes accessed | tf_op | source)
XLA Modules:
  0.0 332.0 jit_solution(17420533623680558351)
XLA Ops:
  0.6 302.5 %train_step.1 = (bf16[18,2,4,192,512]{4,3,2,1,0:T(8,128)(2,1)}, bf16[18,192,512]{2,1,0:T(8,128)(2,1)}) custom-call(bf16[2048,768]{1,0:T(8,128)(2,1)} %bitcast.6, bf16[2048,768]{1,0:T(8,128)(2,1)} %bitcast.7, bf16[2,768,3072]{2,1,0:T(8,128)(2,1)} %wg_hbm.1, bf16[2,768,3072]{2,1,0:T(8,128)(2,1)} %wu_hbm.1, bf16[2,3072,768]{2,1,0:T(8,128)(2,1)} %wd_hbm.1, ...), custom_call_target="tpu_custom_call" | custom-call | tf_op jit(solution)/shard_map/train_step/pallas_call | solution.py:385
  303.1 28.7 %unpack.1 = (bf16[2,768,3072]{2,1,0:T(8,128)(2,1)}, bf16[2,768,3072]{2,1,0:T(8,128)(2,1)}, bf16[2,3072,768]{2,1,0:T(8,128)(2,1)}, f32[2,96,3072]{2,1,0:T(8,128)}...) custom-call(bf16[2,9,2,4,192,512]{5,4,3,2,1,0:T(8,128)(2,1)} %bitcas, ...), custom_call_target="tpu_custom_call" | custom-call | tf_op jit(solution)/shard_map/unpack/pallas_call | solution.py:539

commit v7 on v6

--- a/solution.py
+++ b/solution.py
@@ -8,6 +8,7 @@
 T, D, FF = 2048, 768, 3072
 S = 512
 B = 512
+W = 1024
 TICKS = 8
 R = 192
 NS = 6
@@ -81,8 +82,8 @@
             pltpu.make_async_copy(gbuf.at[slot], gout.at[u], out_sem.at[1, slot]),
         )
 
-    def rows(i):
-        return pl.ds(pl.multiple_of(i * B, B), B)
+    def rows(i, size=B):
+        return pl.ds(pl.multiple_of(i * size, size), size)
 
     def start_weights(jj, half):
         layer, j = 1 - jj // 3, jj % 3
@@ -218,28 +219,31 @@
             def _():
                 send_stage(stage, unit_jj, k)
 
+    def norm_block(i, states):
+        wide = states.astype(F32)
+        value = (wide * scale_of(wide)).astype(BF)
+        a[rows(i), :] = value
+        at[:, rows(i)] = value.T
+
     def norm_states():
         @pl.loop(0, T // B)
         def _(i):
-            wide = h[rows(i), :].astype(F32)
-            value = (wide * scale_of(wide)).astype(BF)
-            a[rows(i), :] = value
-            at[:, rows(i)] = value.T
+            norm_block(i, h[rows(i), :])
 
     def piece_hidden(half):
         wait_weights(half)
 
-        @pl.loop(0, T // B)
+        @pl.loop(0, T // W)
         def _(i):
-            here = a[rows(i), :]
+            here = a[rows(i, W), :]
             gate = nn(here, wgv[half])
             up = nn(here, wuv[half])
-            dact = nt(ct[rows(i), :], wdv[half]).astype(BF).astype(F32)
+            dact = nt(ct[rows(i, W), :], wdv[half]).astype(BF).astype(F32)
             sig = jax.nn.sigmoid(gate)
             silu = gate * sig
-            actt[:, rows(i)] = (silu * up).astype(BF).T
-            dup[half, rows(i), :] = (dact * silu).astype(BF)
-            dgate[half, rows(i), :] = (dact * up * (sig * (1.0 + gate * (1.0 - sig)))).astype(BF)
+            actt[:, rows(i, W)] = (silu * up).astype(BF).T
+            dup[half, rows(i, W), :] = (dact * silu).astype(BF)
+            dgate[half, rows(i, W), :] = (dact * up * (sig * (1.0 + gate * (1.0 - sig)))).astype(BF)
 
     def piece_gate_up(jj, half):
         slot = 3 * (jj % 2) + half
@@ -262,11 +266,11 @@
                 grad[slot, d % 2, d // 2, pl.ds(128, 64), pl.ds(256, 256)] = block[64:, 512:]
 
     def piece_states(half):
-        @pl.loop(0, T // B)
+        @pl.loop(0, T // W)
         def _(i):
-            acc[rows(i), :] += nt(dgate[half, rows(i), :], wgv[half]) + nt(dup[half, rows(i), :], wuv[half])
-
-    def next_layer():
+            acc[rows(i, W), :] += nt(dgate[half, rows(i, W), :], wgv[half]) + nt(dup[half, rows(i, W), :], wuv[half])
+
+    def next_cotangent():
         @pl.loop(0, T // B)
         def _(i):
             wide = h[rows(i), :].astype(F32)
@@ -277,6 +281,7 @@
             ct[rows(i), :] = ct[rows(i), :] + dh
             pltpu.make_async_copy(x_hbm.at[rows(i)], h.at[rows(i)], load_sem.at[0]).start()
 
+    def next_states():
         pltpu.make_async_copy(x_hbm, h, load_sem.at[0]).wait()
         norm_states()
 
@@ -289,25 +294,29 @@
     def piece_forward(half):
         wait_weights(half)
 
-        @pl.loop(0, T // B)
+        @pl.loop(0, T // W)
         def _(i):
-            here = a[rows(i), :]
+            here = a[rows(i, W), :]
             gate = nn(here, wgv[half])
             up = nn(here, wuv[half])
             act = (gate * jax.nn.sigmoid(gate) * up).astype(BF)
-            acc[rows(i), :] += nn(act, wdv[half])
-
-    loads = [pltpu.make_async_copy(x_hbm, h, load_sem.at[0]), pltpu.make_async_copy(dy_hbm, ct, load_sem.at[1])]
-    loads[0].start()
+            acc[rows(i, W), :] += nn(act, wdv[half])
+
+    def load_x(i):
+        return pltpu.make_async_copy(x_hbm.at[rows(i)], h.at[rows(i)], load_sem.at[1 + i])
+
+    load_dy = pltpu.make_async_copy(dy_hbm, ct, load_sem.at[0])
+    for i in range(T // B):
+        load_x(i).start()
     start_forward(0, 0)
-    loads[1].start()
+    load_dy.start()
     barrier = pltpu.get_barrier_semaphore()
     for device in (partner, xn, yn):
         pl.semaphore_signal(barrier, inc=1, device_id=(rep, device), device_id_type=pl.DeviceIdType.MESH)
-    loads[0].wait()
 
     @pl.loop(0, T // B)
     def _(i):
+        load_x(i).wait()
         wide = h[rows(i), :].astype(F32)
         a[rows(i), :] = (wide * scale_of(wide)).astype(BF)
         acc[rows(i), :] = jnp.zeros((B, D), F32)
@@ -329,18 +338,19 @@
 
     @pl.loop(0, T // B)
     def _(i):
-        h[rows(i), :] = h[rows(i), :] + acc[rows(i), :].astype(BF)
+        states = h[rows(i), :] + acc[rows(i), :].astype(BF)
+        h[rows(i), :] = states
         acc[rows(i), :] = jnp.zeros((B, D), F32)
-
-    norm_states()
-    loads[1].wait()
+        norm_block(i, states)
+
+    load_dy.wait()
     pl.semaphore_wait(barrier, 3)
 
     @pl.loop(0, 8)
     def _(jj):
         @pl.when(jj == 3)
         def _():
-            next_layer()
+            next_states()
 
         for half in range(2):
 
@@ -369,6 +379,12 @@
             @pl.when(jj < 3)
             def _():
                 piece_states(half)
+
+            if half == 1:
+
+                @pl.when(jj == 2)
+                def _():
+                    next_cotangent()
 
             if half == 0:
 
@@ -413,7 +429,7 @@
             pltpu.VMEM((NS,) + block, BF),
             pltpu.SemaphoreType.DMA((KINDS, NS)),
             pltpu.SemaphoreType.DMA((KINDS, NS)),
-            pltpu.SemaphoreType.DMA((2,)),
+            pltpu.SemaphoreType.DMA((1 + T // B,)),
             pltpu.SemaphoreType.DMA((2, 3)),
             pltpu.SemaphoreType.DMA((3, 3)),
             pltpu.SemaphoreType.DMA((2, NS)),

time: 332 us -> 325 us (0.979)
  Pallas kernels: 331 us -> 324 us
    pallas_call x1, Pallas kernels: 302 us -> 296 us  [train_step(): pl.pallas_call(step_kernel, out_shape=(jax.ShapeDtypeStruct((UNITS, 2, 4)...]
where the time goes in v7:
time: 325 us
  Pallas kernels  324 us (100%)
    pallas_call x1, Pallas kernels, train_step(): pl.pallas_call(step_kernel, out_shape=(jax.ShapeDtypeStruct((UNITS, 2, 4)...  296 us
    pallas_call x1, Pallas kernels, unpack(): pl.pallas_call(unpack_kernel, out_shape=[jax.ShapeDtypeStruct(s, BF) for...  28.7 us

profile of v7, /device:TPU:0, one launch (start us, length us, event | category | flops | bytes accessed | tf_op | source)
XLA Modules:
  0.0 325.2 jit_solution(10498784193550538115)
XLA Ops:
  0.6 295.7 %train_step.1 = (bf16[18,2,4,192,512]{4,3,2,1,0:T(8,128)(2,1)}, bf16[18,192,512]{2,1,0:T(8,128)(2,1)}) custom-call(bf16[2048,768]{1,0:T(8,128)(2,1)} %bitcast.6, bf16[2048,768]{1,0:T(8,128)(2,1)} %bitcast.7, bf16[2,768,3072]{2,1,0:T(8,128)(2,1)} %wg_hbm.1, bf16[2,768,3072]{2,1,0:T(8,128)(2,1)} %wu_hbm.1, bf16[2,3072,768]{2,1,0:T(8,128)(2,1)} %wd_hbm.1, ...), custom_call_target="tpu_custom_call" | custom-call | tf_op jit(solution)/shard_map/train_step/pallas_call | solution.py:401
  296.3 28.7 %unpack.1 = (bf16[2,768,3072]{2,1,0:T(8,128)(2,1)}, bf16[2,768,3072]{2,1,0:T(8,128)(2,1)}, bf16[2,3072,768]{2,1,0:T(8,128)(2,1)}, f32[2,96,3072]{2,1,0:T(8,128)}...) custom-call(bf16[2,9,2,4,192,512]{5,4,3,2,1,0:T(8,128)(2,1)} %bitcas, ...), custom_call_target="tpu_custom_call" | custom-call | tf_op jit(solution)/shard_map/unpack/pallas_call | solution.py:555
